TPU v7x, 16 devices: a 4x2x1 block of a 4x4x8 slice. The times are simulated.
16 devices in a mesh: dp: 2 (over y, z), wg: 8 (over x, core).
Axes of the slice: x: 4, y: 2, z: 1, core: 2. Of those that a mesh axis runs over, the one named last changes fastest.
The devices are a block of a 4x4x8 slice.
Arguments:
- hidden: bfloat16 [48, 128, 4096], P(('dp', 'wg')), parts along dimension 0
- seq_lens: int32 [48], P(('dp', 'wg')), parts along dimension 0
- route_idx: int32 [6144, 2], P(('dp', 'wg')), parts along dimension 0
- g_attn_in: bfloat16 [4096], P('wg')
- w_query: bfloat16 [4096, 4096], P('wg')
- w_key: bfloat16 [4096, 1024], P('wg')
- w_value: bfloat16 [4096, 1024], P('wg')
- w_attn_out: bfloat16 [4096, 4096], P('wg')
- g_attn_out: bfloat16 [4096], P('wg')
- g_moe_in: bfloat16 [4096], P('wg')
- w_router: bfloat16 [4096, 8], P('wg')
- w_gate: bfloat16 [8, 4096, 1024], P(None, 'wg')
- w_up: bfloat16 [8, 4096, 1024], P(None, 'wg')
- w_down: bfloat16 [8, 1024, 4096], P(None, 'wg')
- g_moe_out: bfloat16 [4096], P('wg')
Outputs:
- output 1: bfloat16 [48, 128, 4096], P(('dp', 'wg')), parts along dimension 0
- output 2: bfloat16 [48, 128, 8, 128], P(('dp', 'wg')), parts along dimension 0
- output 3: bfloat16 [48, 128, 8, 128], P(('dp', 'wg')), parts along dimension 0
There are 2 independent parts. A program takes and returns all parts, laid end to end along the dimension named above; an argument that names none is the same for every part.
All inputs are finite; a program needn't handle non-finite values.
Results may differ from a plain program's by a relative error of at most 0.02.
Values are sent between devices in bfloat16 or wider.
A program may use at most 768 MiB of HBM per device.

v0:
```python
import functools
import jax
import jax.numpy as jnp
from jax import lax
from jax.sharding import PartitionSpec as P

HEAD_DIM = 128
SOFT_CAP = 30.0
NORM_EPS = 1e-5
ROPE_BASE = 10000.0
ATTN_SCALE = HEAD_DIM ** -0.5


def dot_f32(left_op, right_op):
    return jnp.dot(left_op, right_op, preferred_element_type=jnp.float32)


def rms_norm(values, gain_vec):
    values_f32 = values.astype(jnp.float32)
    inv_rms = lax.rsqrt(jnp.mean(values_f32 * values_f32, axis=-1, keepdims=True) + NORM_EPS)
    return values_f32 * inv_rms * gain_vec.astype(jnp.float32)


def rope_tables(seq_len):
    half_dim = HEAD_DIM // 2
    inv_freq = ROPE_BASE ** (-jnp.arange(half_dim, dtype=jnp.float32) * (2.0 / HEAD_DIM))
    angles = jnp.arange(seq_len, dtype=jnp.float32)[:, None] * inv_freq[None, :]
    return jnp.cos(angles)[:, None, :], jnp.sin(angles)[:, None, :]


def apply_rope(values, cos_t, sin_t):
    half_dim = HEAD_DIM // 2
    values_f32 = values.astype(jnp.float32)
    first_half = values_f32[..., :half_dim]
    second_half = values_f32[..., half_dim:]
    return jnp.concatenate([first_half * cos_t - second_half * sin_t, second_half * cos_t + first_half * sin_t], axis=-1).astype(jnp.bfloat16)


def attend_prompt(operands):
    q_rows, k_rows, v_rows, length = operands
    positions = jnp.arange(q_rows.shape[0])
    scores = jnp.einsum('qkgd,skd->kgqs', q_rows, k_rows, preferred_element_type=jnp.float32) * ATTN_SCALE
    scores = SOFT_CAP * jnp.tanh(scores / SOFT_CAP)
    allowed = (positions[None, :] <= positions[:, None]) & (positions[None, :] < length)
    scores = jnp.where(allowed, scores, -1e30)
    attn_probs = jax.nn.softmax(scores, axis=-1).astype(jnp.bfloat16)
    return jnp.einsum('kgqs,skd->qkgd', attn_probs, v_rows, preferred_element_type=jnp.float32).astype(jnp.bfloat16)


def attend_rows(q_proj, k_proj, v_proj, seq_lens):
    n_prompts = seq_lens.shape[0]
    seq_len = q_proj.shape[0] // n_prompts
    n_heads = q_proj.shape[1] // HEAD_DIM
    n_kv = k_proj.shape[1] // HEAD_DIM
    cos_t, sin_t = rope_tables(seq_len)
    q_rope = apply_rope(q_proj.reshape(n_prompts, seq_len, n_heads, HEAD_DIM), cos_t, sin_t)
    k_rope = apply_rope(k_proj.reshape(n_prompts, seq_len, n_kv, HEAD_DIM), cos_t, sin_t)
    v_heads = v_proj.reshape(n_prompts, seq_len, n_kv, HEAD_DIM)
    q_groups = q_rope.reshape(n_prompts, seq_len, n_kv, n_heads // n_kv, HEAD_DIM)
    context = lax.map(attend_prompt, (q_groups, k_rope, v_heads, seq_lens))
    return context.reshape(n_prompts * seq_len, n_heads * HEAD_DIM), k_rope, v_heads


def moe_rows(h_moe, gate_probs, route_idx, w_gate, w_up, w_down):
    top_k = route_idx.shape[1]
    flat_ids = route_idx.reshape(-1)
    pair_order = jnp.argsort(flat_ids, stable=True)
    counts = jnp.bincount(flat_ids, length=w_gate.shape[0]).astype(jnp.int32)
    sorted_rows = jnp.take(h_moe, pair_order // top_k, axis=0)
    gate_act = lax.ragged_dot(sorted_rows, w_gate, counts, preferred_element_type=jnp.float32)
    up_act = lax.ragged_dot(sorted_rows, w_up, counts, preferred_element_type=jnp.float32)
    inner_act = (jax.nn.gelu(gate_act) * up_act).astype(jnp.bfloat16)
    expert_out = lax.ragged_dot(inner_act, w_down, counts, preferred_element_type=jnp.float32)
    pair_out = jnp.take(expert_out, jnp.argsort(pair_order), axis=0).reshape(h_moe.shape[0], top_k, -1)
    return jnp.sum(gate_probs[:, :, None] * pair_out, axis=1)


def solution(mesh):
    row_spec = P(('dp', 'wg'))
    dim0_spec = P('wg', None)
    dim1_spec = P(None, 'wg', None)
    gather_dim0 = functools.partial(lax.all_gather, axis_name='wg', axis=0, tiled=True)
    gather_dim1 = functools.partial(lax.all_gather, axis_name='wg', axis=1, tiled=True)

    def device_fn(hidden, seq_lens, route_idx, g_attn_in, w_query, w_key, w_value, w_attn_out, g_attn_out, g_moe_in, w_router, w_gate, w_up, w_down, g_moe_out):
        n_prompts, seq_len, d_model = hidden.shape
        tok_rows = hidden.reshape(n_prompts * seq_len, d_model)
        h_attn = rms_norm(tok_rows, gather_dim0(g_attn_in)).astype(jnp.bfloat16)
        q_proj = dot_f32(h_attn, gather_dim0(w_query)).astype(jnp.bfloat16)
        k_proj = dot_f32(h_attn, gather_dim0(w_key)).astype(jnp.bfloat16)
        v_proj = dot_f32(h_attn, gather_dim0(w_value)).astype(jnp.bfloat16)
        context_rows, k_rope, v_heads = attend_rows(q_proj, k_proj, v_proj, seq_lens)
        attn_out = dot_f32(context_rows, gather_dim0(w_attn_out))
        mid_rows = (tok_rows.astype(jnp.float32) + rms_norm(attn_out, gather_dim0(g_attn_out))).astype(jnp.bfloat16)
        h_moe = rms_norm(mid_rows, gather_dim0(g_moe_in)).astype(jnp.bfloat16)
        router_probs = jax.nn.softmax(dot_f32(h_moe, gather_dim0(w_router)), axis=-1)
        gate_probs = jnp.take_along_axis(router_probs, route_idx, axis=1)
        moe_out = moe_rows(h_moe, gate_probs, route_idx, gather_dim1(w_gate), gather_dim1(w_up), gather_dim1(w_down))
        y_rows = (mid_rows.astype(jnp.float32) + rms_norm(moe_out, gather_dim0(g_moe_out))).astype(jnp.bfloat16)
        return y_rows.reshape(hidden.shape), k_rope, v_heads

    return jax.shard_map(
        device_fn,
        mesh=mesh,
        in_specs=(row_spec, row_spec, row_spec, P('wg'), dim0_spec, dim0_spec, dim0_spec, dim0_spec, P('wg'), P('wg'), dim0_spec, dim1_spec, dim1_spec, dim1_spec, P('wg')),
        out_specs=(row_spec, row_spec, row_spec),
        check_vma=False,
    )
```

profile of v0, /device:TPU:113, one launch (start us, length us, event | category | flops | bytes accessed | tf_op | source)
XLA Modules:
  0.0 1416.5 jit_solution(11586832383491631122)
XLA Ops:
  7.2 0.7 all-gather.14.cloned.1.call-update
  8.0 0.7 all-gather.12.cloned.1.call-update
  8.9 0.7 all-gather.16.cloned.1.call-update
  11.6 0.7 all-gather.24.cloned.1.call-update
  12.4 20.7 %all-gather = bf16[8,1,512]{2,1,0:T(2,128)(2,1)S(1)} all-gather(bf16[1,1,512]{2,1,0:T(2,128)(2,1)S(1)} %reshape.218), channel_id=1, replica_groups=mesh['dp'=2,'wg'=8] {'wg'}, dimensions={0}, use_global_device_ids=true | all-gather | bytes 9216 | tf_op jit(solution)/shard_map/all_gather | solution.py:88
  33.7 22.3 %all-gather.1 = bf16[8,1,512]{2,1,0:T(2,128)(2,1)S(1)} all-gather(bf16[1,1,512]{2,1,0:T(2,128)(2,1)S(1)} %reshape.220), channel_id=1, replica_groups=mesh['dp'=2,'wg'=8] {'wg'}, dimensions={0}, use_global_device_ids=true | all-gather | bytes 9216 | tf_op jit(solution)/shard_map/all_gather | solution.py:94
  56.6 20.2 %all-gather.2 = bf16[8,1,512]{2,1,0:T(2,128)(2,1)S(1)} all-gather(bf16[1,1,512]{2,1,0:T(2,128)(2,1)S(1)} %reshape.222), channel_id=1, replica_groups=mesh['dp'=2,'wg'=8] {'wg'}, dimensions={0}, use_global_device_ids=true | all-gather | bytes 9216 | tf_op jit(solution)/shard_map/all_gather | solution.py:95
  78.4 6.4 scatter_custom_fusion
  84.8 1.5 ragged-dot-metadata
  86.3 4.4 sort.34
  90.6 4.4 sort.35
  95.0 0.8 broadcast_in_dim.76
  96.5 21.4 %all-gather.3 = bf16[8,1,512]{2,1,0:T(2,128)(2,1)S(1)} all-gather(bf16[1,1,512]{2,1,0:T(2,128)(2,1)S(1)} %reshape.224), channel_id=1, replica_groups=mesh['dp'=2,'wg'=8] {'wg'}, dimensions={0}, use_global_device_ids=true | all-gather | bytes 9216 | tf_op jit(solution)/shard_map/all_gather | solution.py:99
  118.5 23.9 %all_gather.43 = bf16[4096,8]{0,1:T(8,128)(2,1)S(1)} all-gather(bf16[512,8]{0,1:T(8,128)(2,1)} %param.27), channel_id=1, replica_groups=mesh['dp'=2,'wg'=8] {'wg'}, dimensions={0}, use_global_device_ids=true | all-gather | bytes 73728 | tf_op jit(solution)/shard_map/all_gather | solution.py:96
  145.2 2.6 fusion.23
  147.9 7.2 convert_bitcast_fusion.1
  155.5 7.7 fusion.34
  164.0 1.3 pad_maximum_fusion.1
  165.3 96.0 %all-gather.16.cloned.1.call-done = bf16[4096,4096]{1,0:T(8,128)(2,1)} async-done(((bf16[512,4096]{1,0:T(8,128)(2,1)}), bf16[4096,4096]{1,0:T(8,128)(2,1)}) %all-gather.16.cloned.1.call-update) | async-done | bytes 33554448 | tf_op jit(solution)/shard_map/all_gather | solution.py:89
  261.3 18.0 %convert_bitcast_fusion = f32[48,8,32,128]{3,1,2,0:T(8,128)S(1)} fusion(bf16[384,4096]{1,0:T(8,128)(2,1)} %fusion.23, bf16[4096,4096]{1,0:T(8,128)(2,1)} %all-gather.16.cloned.1.call-done), kind=kOutput, calls=%fused_computation.41 | convolution fusion | flops 12888047616 | bytes 42991616 | tf_op jit(solution)/shard_map/dot_general | solution.py:15
  279.3 1.3 copy.70
  280.6 2.5 subtract_convert_fusion
  283.1 1.2 copy.51
  284.3 1.2 copy.52
  285.5 3.3 pad_maximum_fusion
  288.9 31.3 %while.12 = (s32[]{:T(128)}, bf16[3,128,8,4,128]{4,3,2,1,0:T(4,128)(2,1)}, bf16[3,128,8,128]{3,2,1,0:T(8,128)(2,1)S(1)}, s32[3]{0:T(128)S(1)}, bf16[3,128,8,128]...) while((s32[]{:T(128)}, bf16[3,128,8,4,128]{4,3,2,1,0:T(4,128)(2,1)}, ...), condition=%wide.region_4.5_spmd, body=%wide.region_1.4_spmd.sunk | while | flops 272662784 | bytes 12649825 | solution.py:60
  288.9 1.0 constant_dynamic-slice_fusion.3
  291.2 3.5 fusion.66
  294.9 2.0 fusion.67
  297.0 1.0 copy.84
  298.0 1.3 constant_dynamic-update-slice_fusion.2
  299.3 1.0 constant_dynamic-slice_fusion.3
  301.6 3.5 fusion.66
  305.4 2.0 fusion.67
  307.4 1.0 copy.84
  308.4 1.3 constant_dynamic-update-slice_fusion.2
  309.7 1.0 constant_dynamic-slice_fusion.3
  312.1 3.5 fusion.66
  315.8 2.0 fusion.67
  317.9 1.0 copy.84
  318.8 1.3 constant_dynamic-update-slice_fusion.2
  320.2 0.9 copy-done.6
  321.1 6.1 reshape.173
  327.2 89.2 %all-gather.18.cloned.1.call-done = bf16[4096,4096]{1,0:T(8,128)(2,1)} async-done(((bf16[512,4096]{1,0:T(8,128)(2,1)}), bf16[4096,4096]{1,0:T(8,128)(2,1)}) %all-gather.18.cloned.1.call-update) | async-done | bytes 33554448 | tf_op jit(solution)/shard_map/all_gather | solution.py:93
  416.4 21.9 %multiply_reduce_fusion.2 = (f32[384]{0:T(512)S(1)}, f32[384,4096]{1,0:T(8,128)}) fusion(bf16[384,4096]{1,0:T(8,128)(2,1)} %reshape.173, bf16[4096,4096]{1,0:T(8,128)(2,1)} %all-gather.18.cloned.1.call-done), kind=kOutput, calls=%fused_computation.43 | convolution fusion | flops 12888047616 | bytes 42993152 | tf_op jit(solution)/shard_map/dot_general | solution.py:15
  438.3 4.6 fusion.17
  442.9 1.0 fusion.19
  444.5 0.9 fusion.47
  445.6 4.7 gather_fusion.2
  450.7 5.7 gather_fusion
  456.4 6.1 broadcast_select_fusion
  462.5 249.5 %all-gather.20.cloned.1.call-done = bf16[8,4096,1024]{2,1,0:T(8,128)(2,1)} async-done(((bf16[8,512,1024]{2,1,0:T(8,128)(2,1)}), bf16[8,4096,1024]{2,1,0:T(8,128)(2,1)}) %all-gather.20.cloned.1.call-update) | async-done | bytes 67108880 | tf_op jit(solution)/shard_map/all_gather | solution.py:98
  712.0 35.6 %ragged-dot-none.2 = f32[768,1024]{1,0:T(8,128)} custom-call(s32[1]{0:T(128)} %get-tuple-element.85, s32[9]{0:T(128)} %get-tuple-element.86, s32[10]{0:T(128)} %get-tuple-element.87, s32[10]{0:T(128)} %get-tuple-element.88, s32[1]{0:T(128)} %get-tuple-element.85, bf16[768,4096]{1,0:T(8,128)(2,1)} %broadcast_select_fusion, ...), custom_call_target="tpu_custom_call" | custom-call | flops 6442450944 | bytes 76546080 | tf_op jit(solution)/shard_map/ragged_dot_general/ragged-dot-none
  747.6 259.6 %all-gather.22.cloned.1.call-done = bf16[8,4096,1024]{2,1,0:T(8,128)(2,1)} async-done(((bf16[8,512,1024]{2,1,0:T(8,128)(2,1)}), bf16[8,4096,1024]{2,1,0:T(8,128)(2,1)}) %all-gather.22.cloned.1.call-update) | async-done | bytes 67108880 | tf_op jit(solution)/shard_map/all_gather | solution.py:98
  1007.2 35.6 %ragged-dot-none.1 = f32[768,1024]{1,0:T(8,128)} custom-call(s32[1]{0:T(128)} %get-tuple-element.85, s32[9]{0:T(128)} %get-tuple-element.86, s32[10]{0:T(128)} %get-tuple-element.87, s32[10]{0:T(128)} %get-tuple-element.88, s32[1]{0:T(128)} %get-tuple-element.85, bf16[768,4096]{1,0:T(8,128)(2,1)} %broadcast_select_fusion, ...), custom_call_target="tpu_custom_call" | custom-call | flops 6442450944 | bytes 76546080 | tf_op jit(solution)/shard_map/ragged_dot_general/ragged-dot-none
  1042.7 4.2 fusion.33
  1046.9 255.6 %all-gather.24.cloned.1.call-done = bf16[8,1024,4096]{2,1,0:T(8,128)(2,1)} async-done(((bf16[8,128,4096]{2,1,0:T(8,128)(2,1)}), bf16[8,1024,4096]{2,1,0:T(8,128)(2,1)}) %all-gather.24.cloned.1.call-update) | async-done | bytes 67108880 | tf_op jit(solution)/shard_map/all_gather | solution.py:98
  1302.5 38.7 %ragged-dot-none = f32[768,4096]{1,0:T(8,128)} custom-call(s32[1]{0:T(128)} %get-tuple-element.85, s32[9]{0:T(128)} %get-tuple-element.86, s32[10]{0:T(128)} %get-tuple-element.87, s32[10]{0:T(128)} %get-tuple-element.88, s32[1]{0:T(128)} %get-tuple-element.85, bf16[768,1024]{1,0:T(8,128)(2,1)} %fusion.33, bf16[8,1024,4096]{2,1,0:T(8,128)(2,1)} %all-gather.24.cloned.1.call-done), custom_call_target="tpu_custom_call" | custom-call | flops 6442450944 | bytes 81264672 | tf_op jit(solution)/shard_map/ragged_dot_general/ragged-dot-none
  1341.2 16.6 %gather_fusion.1 = f32[768,4096]{1,0:T(8,128)} fusion(f32[768,4096]{1,0:T(8,128)} %ragged-dot-none, s32[1024]{0:T(1024)S(1)} %copy-done.14), kind=kCustom, calls=%fused_computation.1 | custom fusion | bytes 25168896 | tf_op jit(solution)/shard_map/jit(_take)/gather | solution.py:74
  1357.8 15.3 %gather.17 = f32[384,2,4096]{2,1,0:T(2,128)} reshape(f32[768,4096]{1,0:T(8,128)} %gather_fusion.1) | data formatting | bytes 25165824 | tf_op jit(solution)/shard_map/jit(_take)/gather | solution.py:74
  1373.1 28.4 %multiply_reduce_fusion = f32[384,4096]{1,0:T(8,128)} fusion(f32[384,2,4096]{2,1,0:T(2,128)} %gather.17, pred[384,2]{1,0:T(8,128)(4,1)S(1)} %copy-done.7, f32[384,2]{1,0:T(8,128)S(1)} %copy.58), kind=kLoop, calls=%fused_computation.26 | loop fusion | flops 7864320 | bytes 18878208 | tf_op jit(solution)/shard_map/reduce_sum | solution.py:75
  1401.5 3.4 multiply_reduce_fusion.1
  1404.9 1.1 copy-done
  1406.1 3.1 fusion.20
  (105 shorter events, 15.8 us)
Async XLA Ops:
  7.2 140.7 %all-gather.14.cloned.1.call-start = ((), (), s32[]{:S(2)}) async-start(), calls=%async_computation.1 | async-start | bytes 9437184 | tf_op jit(solution)/shard_map/all_gather | solution.py:90
  8.0 147.5 %all-gather.12.cloned.1.call-start = ((), (), s32[]{:S(2)}) async-start(), calls=%async_computation | async-start | bytes 9437184 | tf_op jit(solution)/shard_map/all_gather | solution.py:91
  8.8 252.5 %all-gather.16.cloned.1.call-start = ((), (), s32[]{:S(2)}) async-start(), calls=%async_computation.2 | async-start | bytes 37748736 | tf_op jit(solution)/shard_map/all_gather | solution.py:89
  9.6 406.8 %all-gather.18.cloned.1.call-start = ((), (), s32[]{:S(2)}) async-start(), calls=%async_computation.3 | async-start | bytes 37748736 | tf_op jit(solution)/shard_map/all_gather | solution.py:93
  10.2 701.8 %all-gather.20.cloned.1.call-start = ((), (), s32[]{:S(2)}) async-start(), calls=%async_computation.4 | async-start | bytes 75497472 | tf_op jit(solution)/shard_map/all_gather | solution.py:98
  10.9 996.3 %all-gather.22.cloned.1.call-start = ((), (), s32[]{:S(2)}) async-start(), calls=%async_computation.5 | async-start | bytes 75497472 | tf_op jit(solution)/shard_map/all_gather | solution.py:98
  11.5 0.9 copy-start.17
  11.5 22.2 %copy-start.18 = (bf16[512]{0:T(512)(128)(2,1)S(1)}, bf16[512]{0:T(512)(128)(2,1)}, u32[]{:S(2)}) copy-start(bf16[512]{0:T(512)(128)(2,1)} %param.25) | copy-start | bytes 3076
  11.5 45.1 %copy-start.19 = (bf16[512]{0:T(512)(128)(2,1)S(1)}, bf16[512]{0:T(512)(128)(2,1)}, u32[]{:S(2)}) copy-start(bf16[512]{0:T(512)(128)(2,1)} %param.26) | copy-start | bytes 3076
  11.5 65.9 %copy-start.12 = (s32[384,2]{0,1:T(2,128)S(1)}, s32[384,2]{0,1:T(2,128)}, u32[]{:S(2)}) copy-start(s32[384,2]{0,1:T(2,128)} %param.19) | copy-start | bytes 9220
  11.5 132.7 %copy-start.1 = (bf16[3,128,4096]{2,1,0:T(8,128)(2,1)S(1)}, bf16[3,128,4096]{2,1,0:T(8,128)(2,1)}, u32[]{:S(2)}) copy-start(bf16[3,128,4096]{2,1,0:T(8,128)(2,1)} %param.17) | copy-start | bytes 9437188
  11.6 1290.9 %all-gather.24.cloned.1.call-start = ((), (), s32[]{:S(2)}) async-start(), calls=%async_computation.6 | async-start | bytes 75497472 | tf_op jit(solution)/shard_map/all_gather | solution.py:98
  77.9 67.3 %copy-start.11 = (f32[8,1,512]{2,1,0:T(1,128)S(1)}, f32[8,1,512]{2,1,0:T(1,128)}, u32[]{:S(2)}) copy-start(f32[8,1,512]{2,1,0:T(1,128)} %convert_element_type.103) | copy-start | bytes 49156
  285.5 3.4 copy-start.20
  320.2 0.9 copy-start.6
  327.2 111.0 %copy-start.2 = (bf16[3,128,4096]{2,1,0:T(8,128)(2,1)S(1)}, bf16[3,128,4096]{2,1,0:T(8,128)(2,1)}, u32[]{:S(2)}) copy-start(bf16[3,128,4096]{2,1,0:T(8,128)(2,1)} %param.17) | copy-start | bytes 9437188
  327.2 111.0 %copy-start.10 = (f32[8,1,512]{2,1,0:T(1,128)S(1)}, f32[8,1,512]{2,1,0:T(1,128)}, u32[]{:S(2)}) copy-start(f32[8,1,512]{2,1,0:T(1,128)} %convert_element_type.104) | copy-start | bytes 49156
  438.3 4.6 copy-start.9
  442.9 1.7 copy-start.3
  445.5 5.0 copy-start.13
  445.5 5.1 copy-start.15
  450.7 5.7 copy-start.16
  747.6 295.1 %copy-start.5 = (f32[768,1024]{1,0:T(8,128)S(1)}, f32[768,1024]{1,0:T(8,128)}, u32[]{:S(2)}) copy-start(f32[768,1024]{1,0:T(8,128)} %ragged-dot-none.2) | copy-start | bytes 9437188
  1046.9 294.2 %copy-start.14 = (s32[1024]{0:T(1024)S(1)}, s32[1024]{0:T(1024)}, u32[]{:S(2)}) copy-start(s32[1024]{0:T(1024)} %pad_clamp_fusion) | copy-start | bytes 12292
  1357.8 15.3 %copy-start.7 = (pred[384,2]{1,0:T(8,128)(4,1)S(1)}, pred[384,2]{1,0:T(8,128)(4,1)}, u32[]{:S(2)}) copy-start(pred[384,2]{1,0:T(8,128)(4,1)} %broadcast_in_dim.76) | copy-start | bytes 2308
  1373.1 31.8 %copy-start.4 = (bf16[384,4096]{1,0:T(8,128)(2,1)S(1)}, bf16[384,4096]{1,0:T(8,128)(2,1)}, u32[]{:S(2)}) copy-start(bf16[384,4096]{1,0:T(8,128)(2,1)} %copy-done.3) | copy-start | bytes 9437188
  1373.1 31.8 %copy-start.8 = (f32[8,1,512]{2,1,0:T(1,128)S(1)}, f32[8,1,512]{2,1,0:T(1,128)}, u32[]{:S(2)}) copy-start(f32[8,1,512]{2,1,0:T(1,128)} %convert_element_type.106) | copy-start | bytes 49156
  1401.5 4.6 copy-start
Sparse Core Ops, SparseCore 0:
  9.6 49.0 all-gather.13
  60.3 45.7 all-gather.11
  107.7 153.5 all-gather.15
  262.7 153.5 all-gather.17
  417.8 294.1 all-gather.19
  713.4 293.6 all-gather.21
  1008.7 293.6 all-gather.23
where the time goes:
time: 1420 us
  waiting for transfers between devices  954 us (67%)
  Pallas kernels  111 us (8%)
  blocking collectives  108 us (8%)
  other arithmetic  83.8 us (6%)
  matrix products  72.4 us (5%)
  local copies, waits for them, and re-layouts  70.5 us (5%)
  between operations  15 us (1%)
    all_gather x1, waiting for transfers between devices, device_fn(): gather_dim1(w_up)  260 us
    all_gather x1, waiting for transfers between devices, device_fn(): gather_dim1(w_down)  256 us
    all_gather x1, waiting for transfers between devices, device_fn(): gather_dim1(w_gate)  249 us
    another operation x3, Pallas kernels  110 us
    all_gather x1, waiting for transfers between devices, device_fn(): q_proj = dot_f32(h_attn, gather_dim0(w_query)).astype(jnp.bfloat16)  96 us
    all_gather x1, waiting for transfers between devices, device_fn(): attn_out = dot_f32(context_rows, gather_dim0(w_attn_out))  89.2 us
    dot_general x5, matrix products, dot_f32(): return jnp.dot(left_op, right_op, preferred_element_type=jnp.float32)  55.7 us
    gather x2, local copies, waits for them, and re-layouts, moe_rows(): jnp.take(expert_out, jnp.argsort(pair_order), axis=0)  31.9 us
  transfers between devices with their start and end apart: 7, of which 5 were waited for; matrix products, arithmetic and copies ran while one was open for 11% of the time, Pallas kernels for 5%

commit v1 on v0

--- a/solution.py
+++ b/solution.py
@@ -2,13 +2,20 @@
 import jax
 import jax.numpy as jnp
 from jax import lax
+from jax.experimental import pallas as pl
+from jax.experimental.pallas import tpu as pltpu
 from jax.sharding import PartitionSpec as P
 
 HEAD_DIM = 128
+LANES = 128
 SOFT_CAP = 30.0
 NORM_EPS = 1e-5
 ROPE_BASE = 10000.0
 ATTN_SCALE = HEAD_DIM ** -0.5
+MESH = pl.DeviceIdType.MESH
+ANY = pl.BlockSpec(memory_space=pl.ANY)
+VMEM_FULL = pl.BlockSpec(memory_space=pltpu.VMEM)
+DIRS = (1, -1)
 
 
 def dot_f32(left_op, right_op):
@@ -61,42 +68,480 @@
     return context.reshape(n_prompts * seq_len, n_heads * HEAD_DIM), k_rope, v_heads
 
 
-def moe_rows(h_moe, gate_probs, route_idx, w_gate, w_up, w_down):
-    top_k = route_idx.shape[1]
-    flat_ids = route_idx.reshape(-1)
-    pair_order = jnp.argsort(flat_ids, stable=True)
-    counts = jnp.bincount(flat_ids, length=w_gate.shape[0]).astype(jnp.int32)
-    sorted_rows = jnp.take(h_moe, pair_order // top_k, axis=0)
-    gate_act = lax.ragged_dot(sorted_rows, w_gate, counts, preferred_element_type=jnp.float32)
-    up_act = lax.ragged_dot(sorted_rows, w_up, counts, preferred_element_type=jnp.float32)
-    inner_act = (jax.nn.gelu(gate_act) * up_act).astype(jnp.bfloat16)
-    expert_out = lax.ragged_dot(inner_act, w_down, counts, preferred_element_type=jnp.float32)
-    pair_out = jnp.take(expert_out, jnp.argsort(pair_order), axis=0).reshape(h_moe.shape[0], top_k, -1)
-    return jnp.sum(gate_probs[:, :, None] * pair_out, axis=1)
+class Place:
+    def __init__(self, n):
+        self.n = n
+        self.chips = n // 2
+        self.me = lax.axis_index('wg')
+        self.dp = lax.axis_index('dp')
+        self.chip = self.me // 2
+        self.core = self.me % 2
+        self.parity = self.dp % 2
+        self.twin = self.dp + 1 - 2 * self.parity
+
+    def at(self, offset, rel):
+        return ((self.chip + offset + self.chips) % self.chips) * 2 + (self.core + rel) % 2
+
+    def chip_at(self, offset):
+        return (self.chip + offset + self.chips) % self.chips
+
+
+class Wires:
+    def __init__(self, place, send_sems, recv_sems):
+        self.place, self.send_sems, self.recv_sems = place, send_sems, recv_sems
+        self.slots = {}
+        self.open = []
+
+    def copy(self, name, src, dst, wg=None, dp=None):
+        slot = self.slots.setdefault(name, len(self.slots))
+        return pltpu.make_async_remote_copy(
+            src_ref=src, dst_ref=dst, send_sem=self.send_sems.at[slot], recv_sem=self.recv_sems.at[slot],
+            device_id={'dp': self.place.dp if dp is None else dp, 'wg': self.place.me if wg is None else wg},
+            device_id_type=MESH)
+
+    def send(self, name, src, dst, wg=None, dp=None):
+        desc = self.copy(name, src, dst, wg, dp)
+        desc.start()
+        self.open.append(desc)
+
+    def recv(self, name, dst):
+        self.copy(name, dst, dst).wait_recv()
+
+    def finish(self):
+        for desc in self.open:
+            desc.wait_send()
+        self.open = []
+
+
+def enter(place, with_twin):
+    barrier = pltpu.get_barrier_semaphore()
+    peers = [(place.dp, place.at(off, rel)) for off in DIRS for rel in (0, 1)] + [(place.dp, place.at(0, 1))]
+    if with_twin:
+        peers.append((place.twin, place.me))
+    for dp, wg in peers:
+        pl.semaphore_signal(barrier, inc=1, device_id={'dp': dp, 'wg': wg}, device_id_type=MESH)
+    pl.semaphore_wait(barrier, len(peers))
+
+
+def reshard_kernel(n, gate, up, down, wgu, wd, relay_gu, relay_d, send_sems, recv_sems, loc_sems):
+    place = Place(n)
+    wires = Wires(place, send_sems, recv_sems)
+    experts, rows, cols = gate.shape[0], gate.shape[1], gate.shape[2] // n
+    drows, dcols = down.shape[1], down.shape[2] // n
+    half, quarter = experts // 2, experts // 4
+    mine, theirs = place.parity * half, half - place.parity * half
+    me = place.me
+
+    def piece(arr, e0, cnt, j):
+        if arr == 'd':
+            return down.at[pl.ds(e0, cnt), :, pl.ds(pl.multiple_of(j * dcols, LANES), dcols)]
+        return (gate if arr == 'g' else up).at[pl.ds(e0, cnt), :, pl.ds(pl.multiple_of(j * cols, LANES), cols)]
+
+    def land(arr, e0, cnt, src):
+        if arr == 'd':
+            return wd.at[pl.ds(e0, cnt), pl.ds(pl.multiple_of(src * drows, drows), drows), :]
+        row = pl.ds(pl.multiple_of(src * rows, rows), rows)
+        if arr == 'gu':
+            return wgu.at[pl.ds(e0, cnt), row, :]
+        return wgu.at[pl.ds(e0, cnt), row, pl.ds(0 if arr == 'g' else cols, cols)]
+
+    def relay(arr, side, rel):
+        if arr == 'd':
+            return relay_d.at[side, rel]
+        if arr == 'gu':
+            return relay_gu.at[side, rel]
+        return relay_gu.at[side, rel, :, :, pl.ds(0 if arr == 'g' else cols, cols)]
+
+    enter(place, True)
+    local = []
+    for i, arr in enumerate('gud'):
+        desc = pltpu.make_async_copy(piece(arr, 0, experts, me), land(arr, 0, experts, me), loc_sems.at[i])
+        desc.start()
+        local.append(desc)
+
+    def direct(rel, arrs):
+        for arr in arrs:
+            for d in DIRS:
+                to = place.at(d, rel)
+                wires.send(('direct', d, rel, arr), piece(arr, mine, half, to), land(arr, mine, half, me), wg=to)
+
+    def first_leg(rel, arrs):
+        for arr in arrs:
+            for side, d in enumerate(DIRS):
+                e0 = mine + side * quarter
+                wires.send(('leg1', d, rel, arr), piece(arr, e0, quarter, place.at(2 * d, rel)), relay(arr, side, rel),
+                           wg=place.at(d, 0))
+
+    def to_twin(name, arr, e0, cnt, src):
+        region = land(arr, e0, cnt, src)
+        wires.send(name, region, region, dp=place.twin)
+
+    direct(0, 'gud')
+    sib = place.at(0, 1)
+    for arr in 'gud':
+        wires.send(('sib', arr), piece(arr, 0, experts, sib), land(arr, 0, experts, me), wg=sib)
+    first_leg(0, 'gud')
+    first_leg(1, 'gud')
+    direct(1, 'gud')
+
+    def direct_in(rel, arrs):
+        for arr in arrs:
+            for d in DIRS:
+                src = place.at(-d, rel)
+                if arr == 'gu':
+                    wires.recv(('direct', d, rel, 'g'), land('g', mine, half, src))
+                    wires.recv(('direct', d, rel, 'u'), land('u', mine, half, src))
+                else:
+                    wires.recv(('direct', d, rel, arr), land(arr, mine, half, src))
+                to_twin(('twin', d, rel, arr), arr, mine, half, src)
+
+    def second_leg(rel):
+        for arr in ('gu', 'd'):
+            for side, d in enumerate(DIRS):
+                if arr == 'gu':
+                    wires.recv(('leg1', d, rel, 'g'), relay('g', side, rel))
+                    wires.recv(('leg1', d, rel, 'u'), relay('u', side, rel))
+                else:
+                    wires.recv(('leg1', d, rel, arr), relay(arr, side, rel))
+                wires.send(('leg2', d, rel, arr), relay(arr, side, rel), land(arr, mine + side * quarter, quarter, place.at(-d, 0)),
+                           wg=place.at(d, rel))
+
+    direct_in(0, ('gu', 'd'))
+    second_leg(0)
+    second_leg(1)
+    direct_in(1, ('gu', 'd'))
+    for rel in (0, 1):
+        for arr in ('gu', 'd'):
+            for side, d in enumerate(DIRS):
+                src = place.at(2 * d, rel)
+                e0 = mine + side * quarter
+                wires.recv(('leg2', d, rel, arr), land(arr, e0, quarter, src))
+                to_twin(('twin2', d, rel, arr), arr, e0, quarter, src)
+    for arr in 'gud':
+        wires.recv(('sib', arr), land(arr, 0, experts, sib))
+    for rel in (0, 1):
+        for arr in ('gu', 'd'):
+            for side, d in enumerate(DIRS):
+                wires.recv(('twin', d, rel, arr), land(arr, theirs, half, place.at(-d, rel)))
+                wires.recv(('twin2', d, rel, arr), land(arr, theirs + side * quarter, quarter, place.at(2 * d, rel)))
+    for desc in local:
+        desc.wait()
+    wires.finish()
+
+
+def reshard(n, gate, up, down):
+    experts, rows, ff = gate.shape
+    drows, d_model = down.shape[1:]
+    cols, dcols = ff // n, d_model // n
+    bf16 = jnp.bfloat16
+    outs = pl.pallas_call(
+        functools.partial(reshard_kernel, n),
+        name='reshard',
+        out_shape=(
+            jax.ShapeDtypeStruct((experts, rows * n, 2 * cols), bf16),
+            jax.ShapeDtypeStruct((experts, drows * n, dcols), bf16),
+            jax.ShapeDtypeStruct((2, 2, experts // 4, rows, 2 * cols), bf16),
+            jax.ShapeDtypeStruct((2, 2, experts // 4, drows, dcols), bf16),
+        ),
+        in_specs=[ANY] * 3,
+        out_specs=(ANY,) * 4,
+        scratch_shapes=[pltpu.SemaphoreType.DMA((64,)), pltpu.SemaphoreType.DMA((64,)), pltpu.SemaphoreType.DMA((4,))],
+        compiler_params=pltpu.CompilerParams(collective_id=0, has_side_effects=True),
+        cost_estimate=pl.CostEstimate(flops=100_000_000_000, bytes_accessed=50_000_000, transcendentals=0),
+    )(gate, up, down)
+    return outs[0], outs[1]
+
+
+class Gather:
+    def __init__(self, wires, name, region, half_region):
+        self.wires, self.place, self.name = wires, wires.place, name
+        self.region, self.half_region = region, half_region
+
+    def start(self, src):
+        place, dst = self.place, self.region(self.place.me)
+        for d in DIRS:
+            self.wires.send((self.name, 'own', d), src, dst, wg=place.at(d, 0))
+        self.wires.send((self.name, 'own', 0), src, dst, wg=place.at(0, 1))
+
+    def near_in(self, side):
+        d, place = DIRS[side], self.place
+        owner = place.at(-d, 0)
+        block, part = self.region(owner), self.half_region(owner, side)
+        self.wires.recv((self.name, 'own', d), block)
+        self.wires.send((self.name, 'far', d), part, part, wg=place.at(d, 0))
+        self.wires.send((self.name, 'across', d), block, block, wg=place.at(0, 1))
+
+    def far_in(self):
+        place = self.place
+        owner = place.at(2, 0)
+        for side, d in enumerate(DIRS):
+            part = self.half_region(owner, side)
+            self.wires.recv((self.name, 'far', d), part)
+            self.wires.send((self.name, 'across2', d), part, part, wg=place.at(0, 1))
+
+    def sib_own(self):
+        self.wires.recv((self.name, 'own', 0), self.region(self.place.at(0, 1)))
+
+    def sib_near(self, side):
+        self.wires.recv((self.name, 'across', DIRS[side]), self.region(self.place.at(-DIRS[side], 1)))
+
+    def sib_far(self):
+        for side, d in enumerate(DIRS):
+            self.wires.recv((self.name, 'across2', d), self.half_region(self.place.at(2, 1), side))
+
+
+def moe_kernel(n, experts, h2, route, wr, wgu, wd, m_out, hg, relay_m,
+               vgu, vd, hbuf, u_all, gates, us, mbuf, send_sems, recv_sems, load_sems, w_sems, out_sems):
+    place = Place(n)
+    wires = Wires(place, send_sems, recv_sems)
+    steps, seq, d_model = h2.shape
+    chips, me = place.chips, place.me
+    cols = vgu.shape[2] // 2
+    dcols = vd.shape[2]
+    offsets = (0, -1, 1, 2)
+
+    enter(place, False)
+    h_gathers = []
+    for t in range(steps):
+        gather = Gather(wires, ('h', t), lambda owner, t=t: hg.at[t, owner],
+                        lambda owner, side, t=t: hg.at[t, owner, pl.ds(side * (seq // 2), seq // 2), :])
+        gather.start(h2.at[t])
+        h_gathers.append(gather)
+    w_loads = []
+    for e in range(experts):
+        desc = pltpu.make_async_copy(wgu.at[e], vgu.at[e], w_sems.at[e])
+        desc.start()
+        w_loads.append(desc)
+    d_load = pltpu.make_async_copy(wd, vd, w_sems.at[experts])
+    d_load.start()
+
+    def u_owner_chip(owner, q):
+        return (owner // 2 + offsets[q] + chips) % chips
+
+    u_gathers = {}
+
+    def fetch(t, q, slot):
+        if q == 0:
+            first = pltpu.make_async_copy(h2.at[t], hbuf.at[slot, place.core], load_sems.at[slot, 0])
+            sib = 1 - place.core
+            second = pltpu.make_async_copy(hg.at[t, place.at(0, 1)], hbuf.at[slot, sib], load_sems.at[slot, 1])
+            return [first, second]
+        chip = place.chip_at(offsets[q])
+        return [pltpu.make_async_copy(hg.at[t, pl.ds(2 * chip, 2)], hbuf.at[slot], load_sems.at[slot, 0])]
+
+    def arrive(t, q):
+        gather = h_gathers[t]
+        if q == 0:
+            gather.sib_own()
+        elif q < 3:
+            gather.near_in(q - 1)
+            gather.sib_near(q - 1)
+        else:
+            gather.far_in()
+            gather.sib_far()
+
+    def up_part(t, q, slot):
+        chip = place.chip_at(offsets[q])
+        h = hbuf.at[slot]
+        rows = 2 * seq
+        r0 = route[t, pl.ds(2 * chip, 2), 0].reshape(rows, LANES).astype(jnp.float32)
+        r1 = route[t, pl.ds(2 * chip, 2), 1].reshape(rows, LANES).astype(jnp.float32)
+        logits = dot_f32(h[...].reshape(rows, d_model), wr[...])
+        lane = lax.broadcasted_iota(jnp.int32, (rows, LANES), 1)
+        logits = jnp.where(lane < experts, logits, -1e30)
+        peak = jnp.max(logits, axis=-1, keepdims=True)
+        ex = jnp.where(lane < experts, jnp.exp(logits - peak), 0.0)
+        probs = ex / jnp.sum(ex, axis=-1, keepdims=True)
+        lane_f = lane.astype(jnp.float32)
+        for i, r in enumerate((r0, r1)):
+            g = jnp.sum(jnp.where(lane_f == r, probs, 0.0), axis=-1, keepdims=True)
+            gates[t, chip, i] = jnp.broadcast_to(g, (rows, LANES))
+
+        def expert(e, carry):
+            act = dot_f32(h[...].reshape(rows, d_model), vgu[e])
+            inner = (jax.nn.gelu(act[:, :cols]) * act[:, cols:]).astype(jnp.bfloat16).astype(jnp.float32)
+            e_f = e.astype(jnp.float32)
+            us[0] = jnp.where(route[t, pl.ds(2 * chip, 2), 0].reshape(rows, LANES).astype(jnp.float32) == e_f, inner, us[0])
+            us[1] = jnp.where(route[t, pl.ds(2 * chip, 2), 1].reshape(rows, LANES).astype(jnp.float32) == e_f, inner, us[1])
+            return carry
+
+        us[...] = jnp.zeros_like(us)
+        lax.fori_loop(0, experts, expert, 0)
+        for i in range(2):
+            u_all[t, chip, me, :, pl.ds(i * cols, cols)] = us[i].astype(jnp.bfloat16)
+        gather = Gather(wires, ('u', t, q), lambda owner: u_all.at[t, u_owner_chip(owner, q), owner],
+                        lambda owner, side: u_all.at[t, u_owner_chip(owner, q), owner, pl.ds(side * seq, seq), :])
+        gather.start(u_all.at[t, chip, me])
+        u_gathers[t, q] = gather
+
+    def phase_a(t):
+        for q in range(4):
+            arrive(t, q)
+            loads = fetch(t, q, q % 2)
+            for desc in loads:
+                desc.start()
+            for desc in loads:
+                desc.wait()
+            if t == 0 and q == 0:
+                for desc in w_loads:
+                    desc.wait()
+            up_part(t, q, q % 2)
+
+    def u_near(t):
+        for q in range(4):
+            u_gathers[t, q].near_in(0)
+            u_gathers[t, q].near_in(1)
+
+    m_open = []
+
+    def phase_b(t):
+        if t == 0:
+            d_load.wait()
+        for q in range(4):
+            gather = u_gathers[t, q]
+            gather.far_in()
+            gather.sib_own()
+            gather.sib_near(0)
+            gather.sib_near(1)
+            gather.sib_far()
+        for q in range(4):
+            chip = place.chip_at(offsets[q])
+            rows = 2 * seq
+            acc = mbuf.at[t, q]
+            acc[...] = jnp.zeros_like(acc)
+
+            def expert(e, carry):
+                e_b = e.astype(jnp.bfloat16)
+                r0 = route[t, pl.ds(2 * chip, 2), 0].reshape(rows, LANES)
+                r1 = route[t, pl.ds(2 * chip, 2), 1].reshape(rows, LANES)
+                m0, m1 = r0 == e_b, r1 == e_b
+                zero = jnp.zeros((rows, LANES), jnp.bfloat16)
+                parts = []
+                for j in range(n):
+                    parts.append(jnp.where(m0, u_all[t, chip, j, :, pl.ds(0, cols)],
+                                           jnp.where(m1, u_all[t, chip, j, :, pl.ds(cols, cols)], zero)))
+                ue = jnp.concatenate(parts, axis=1)
+                out = dot_f32(ue, vd[e])
+                e_f = e.astype(jnp.float32)
+                gate = jnp.where(r0.astype(jnp.float32) == e_f, gates[t, chip, 0],
+                                 jnp.where(r1.astype(jnp.float32) == e_f, gates[t, chip, 1], 0.0))
+                acc[...] += jnp.concatenate([gate] * (dcols // LANES), axis=1) * out
+                return carry
+
+            lax.fori_loop(0, experts, expert, 0)
+            own_cols = pl.ds(pl.multiple_of(me * dcols, LANES), dcols)
+            dst = m_out.at[t, :, own_cols]
+            for rel in (0, 1):
+                target_core = (place.core + rel) % 2
+                part = acc.at[pl.ds(pl.multiple_of(target_core * seq, seq), seq), :]
+                if q == 0 and rel == 0:
+                    desc = pltpu.make_async_copy(part, dst, out_sems.at[t])
+                    desc.start()
+                    m_open.append(desc)
+                elif q < 3:
+                    wires.send(('m', t, q, rel), part, dst, wg=place.at(offsets[q], rel))
+                else:
+                    wires.send(('m1', t, rel), part, relay_m.at[t, rel], wg=place.at(DIRS[rel], 0))
+
+    def m_relay(t):
+        for rel, d in enumerate(DIRS):
+            wires.recv(('m1', t, rel), relay_m.at[t, rel])
+            src = place.at(-d, 0)
+            wires.send(('m2', t, rel), relay_m.at[t, rel], m_out.at[t, :, pl.ds(pl.multiple_of(src * dcols, LANES), dcols)],
+                       wg=place.at(d, rel))
+
+    def m_in(t):
+        for q in range(4):
+            for rel in (0, 1):
+                src = place.at(-offsets[q], rel)
+                dst = m_out.at[t, :, pl.ds(pl.multiple_of(src * dcols, LANES), dcols)]
+                if q == 0 and rel == 0:
+                    continue
+                wires.recv(('m', t, q, rel) if q < 3 else ('m2', t, rel), dst)
+
+    phase_a(0)
+    for t in range(1, steps):
+        phase_a(t)
+        u_near(t - 1)
+    phase_b(0)
+    u_near(steps - 1)
+    for t in range(1, steps):
+        phase_b(t)
+        m_relay(t - 1)
+    m_relay(steps - 1)
+    for t in range(steps):
+        m_in(t)
+    for desc in m_open:
+        desc.wait()
+    wires.finish()
+
+
+def moe(n, h2, route, wr, wgu, wd):
+    steps, seq, d_model = h2.shape
+    experts, _, two_cols = wgu.shape
+    ff, dcols = wd.shape[1:]
+    bf16, f32 = jnp.bfloat16, jnp.float32
+    n_sems = steps * 64
+    outs = pl.pallas_call(
+        functools.partial(moe_kernel, n, experts),
+        name='moe',
+        out_shape=(
+            jax.ShapeDtypeStruct((steps, seq, d_model), f32),
+            jax.ShapeDtypeStruct((steps, n, seq, d_model), bf16),
+            jax.ShapeDtypeStruct((steps, 2, seq, dcols), f32),
+        ),
+        in_specs=[ANY, VMEM_FULL, VMEM_FULL, ANY, ANY],
+        out_specs=(ANY,) * 3,
+        scratch_shapes=[
+            pltpu.VMEM((experts, d_model, two_cols), bf16),
+            pltpu.VMEM((experts, ff, dcols), bf16),
+            pltpu.VMEM((2, 2, seq, d_model), bf16),
+            pltpu.VMEM((steps, n // 2, n, 2 * seq, two_cols), bf16),
+            pltpu.VMEM((steps, n // 2, 2, 2 * seq, LANES), f32),
+            pltpu.VMEM((2, 2 * seq, two_cols // 2), f32),
+            pltpu.VMEM((steps, 4, 2 * seq, dcols), f32),
+            pltpu.SemaphoreType.DMA((n_sems,)),
+            pltpu.SemaphoreType.DMA((n_sems,)),
+            pltpu.SemaphoreType.DMA((2, 2)),
+            pltpu.SemaphoreType.DMA((experts + 1,)),
+            pltpu.SemaphoreType.DMA((steps,)),
+        ],
+        compiler_params=pltpu.CompilerParams(collective_id=1, has_side_effects=True, vmem_limit_bytes=66_000_000),
+        cost_estimate=pl.CostEstimate(flops=77_000_000_000, bytes_accessed=100_000_000, transcendentals=0),
+    )(h2, route, wr, wgu, wd)
+    return outs[0]
 
 
 def solution(mesh):
+    n = mesh.shape['wg']
     row_spec = P(('dp', 'wg'))
     dim0_spec = P('wg', None)
     dim1_spec = P(None, 'wg', None)
     gather_dim0 = functools.partial(lax.all_gather, axis_name='wg', axis=0, tiled=True)
-    gather_dim1 = functools.partial(lax.all_gather, axis_name='wg', axis=1, tiled=True)
 
     def device_fn(hidden, seq_lens, route_idx, g_attn_in, w_query, w_key, w_value, w_attn_out, g_attn_out, g_moe_in, w_router, w_gate, w_up, w_down, g_moe_out):
         n_prompts, seq_len, d_model = hidden.shape
+        experts = w_router.shape[1]
+        small = jnp.concatenate([w_router] + [g[:, None] for g in (g_attn_in, g_attn_out, g_moe_in, g_moe_out)], axis=1)
+        small = gather_dim0(small)
+        g_attn_in, g_attn_out, g_moe_in, g_moe_out = (small[:, experts + i] for i in range(4))
+        wr = jnp.pad(small[:, :experts], ((0, 0), (0, LANES - experts)))
+        route = lax.all_gather(route_idx, 'wg', axis=0, tiled=False)
+        route = route.reshape(n, n_prompts, seq_len, 2).transpose(1, 0, 3, 2).astype(jnp.bfloat16)
+        route = jnp.broadcast_to(route[..., None], route.shape + (LANES,))
+        wgu, wd = reshard(n, w_gate, w_up, w_down)
+
         tok_rows = hidden.reshape(n_prompts * seq_len, d_model)
-        h_attn = rms_norm(tok_rows, gather_dim0(g_attn_in)).astype(jnp.bfloat16)
+        h_attn = rms_norm(tok_rows, g_attn_in).astype(jnp.bfloat16)
         q_proj = dot_f32(h_attn, gather_dim0(w_query)).astype(jnp.bfloat16)
         k_proj = dot_f32(h_attn, gather_dim0(w_key)).astype(jnp.bfloat16)
         v_proj = dot_f32(h_attn, gather_dim0(w_value)).astype(jnp.bfloat16)
         context_rows, k_rope, v_heads = attend_rows(q_proj, k_proj, v_proj, seq_lens)
         attn_out = dot_f32(context_rows, gather_dim0(w_attn_out))
-        mid_rows = (tok_rows.astype(jnp.float32) + rms_norm(attn_out, gather_dim0(g_attn_out))).astype(jnp.bfloat16)
-        h_moe = rms_norm(mid_rows, gather_dim0(g_moe_in)).astype(jnp.bfloat16)
-        router_probs = jax.nn.softmax(dot_f32(h_moe, gather_dim0(w_router)), axis=-1)
-        gate_probs = jnp.take_along_axis(router_probs, route_idx, axis=1)
-        moe_out = moe_rows(h_moe, gate_probs, route_idx, gather_dim1(w_gate), gather_dim1(w_up), gather_dim1(w_down))
-        y_rows = (mid_rows.astype(jnp.float32) + rms_norm(moe_out, gather_dim0(g_moe_out))).astype(jnp.bfloat16)
+        mid_rows = (tok_rows.astype(jnp.float32) + rms_norm(attn_out, g_attn_out)).astype(jnp.bfloat16)
+        h_moe = rms_norm(mid_rows, g_moe_in).astype(jnp.bfloat16)
+        moe_out = moe(n, h_moe.reshape(hidden.shape), route, wr, wgu, wd).reshape(tok_rows.shape)
+        y_rows = (mid_rows.astype(jnp.float32) + rms_norm(moe_out, g_moe_out)).astype(jnp.bfloat16)
         return y_rows.reshape(hidden.shape), k_rope, v_heads
 
     return jax.shard_map(

time: 1420 us -> 880 us (0.62)
  waiting for transfers between devices: 954 us -> 83 us
  Pallas kernels: 111 us -> 594 us
  blocking collectives: 108 us -> 48.6 us
  other arithmetic: 83.8 us -> 33.2 us
  local copies, waits for them, and re-layouts: 70.5 us -> 28 us
    all_gather x3 -> x0, waiting for transfers between devices: 765 us -> none  [the longest x1 260 us: device_fn(): gather_dim1(w_up)]
    pallas_call x0 -> x2, Pallas kernels: none -> 594 us  [the longest x1 305 us: reshard(): pl.pallas_call(functools.partial(reshard_kernel, n), name='reshard', out_...]
    another operation x3 -> x0, Pallas kernels: 110 us -> none
    all_gather x1, waiting for transfers between devices: 96 us -> 0.01 us  [device_fn(): q_proj = dot_f32(h_attn, gather_dim0(w_query)).astype(jnp.bfloat16)]
    all_gather x5 -> x2, blocking collectives: 108 us -> 48.6 us  [the longest x1 27.7 us: device_fn(): small = gather_dim0(small)]
    gather x8 -> x0, local copies, waits for them, and re-layouts: 42.8 us -> none  [the longest x2 31.9 us: moe_rows(): jnp.take(expert_out, jnp.argsort(pair_order), axis=0)]
    reduce_sum x2 -> x0, other arithmetic: 28.4 us -> none  [the longest x1 28.4 us: moe_rows(): return jnp.sum(gate_probs[:, :, None] * pair_out, axis=1)]
    dot_general x5 -> x4, matrix products: 55.7 us -> 53.6 us  [dot_f32(): return jnp.dot(left_op, right_op, preferred_element_type=jnp.float32)]
  transfers between devices with their start and end apart: 7 -> 4, of which waited for: 5 -> 1; matrix products, arithmetic and copies ran while one was open for 11% -> 10% of each run, Pallas kernels for 5% -> 35%
where the time goes in v1:
time: 880 us; the launch traced here: 872 us
  Pallas kernels  594 us (68%)
  waiting for transfers between devices  83 us (9%)
  matrix products  70.4 us (8%)
  blocking collectives  48.6 us (6%)
  other arithmetic  33.2 us (4%)
  local copies, waits for them, and re-layouts  28 us (3%)
  between operations  14.6 us (2%)
    pallas_call x1, Pallas kernels, reshard(): pl.pallas_call(functools.partial(reshard_kernel, n), name='reshard', out_...  305 us
    pallas_call x1, Pallas kernels, moe(): pl.pallas_call(functools.partial(moe_kernel, n, experts), name='moe', out...  289 us
    all_gather x1, waiting for transfers between devices, device_fn(): attn_out = dot_f32(context_rows, gather_dim0(w_attn_out))  80.2 us
    dot_general x4, matrix products, dot_f32(): return jnp.dot(left_op, right_op, preferred_element_type=jnp.float32)  53.6 us
    all_gather x1, blocking collectives, device_fn(): small = gather_dim0(small)  27.7 us
    all_gather x1, blocking collectives, device_fn(): route = lax.all_gather(route_idx, 'wg', axis=0, tiled=False)  20.9 us
  transfers between devices with their start and end apart: 4, of which 1 were waited for; matrix products, arithmetic and copies ran while one was open for 10% of the time, Pallas kernels for 35%

profile of v1, /device:TPU:113, one launch (start us, length us, event | category | flops | bytes accessed | tf_op | source)
XLA Modules:
  0.0 871.9 jit_solution(8100151246655851295)
XLA Ops:
  7.2 0.7 all-gather.8.cloned.1.call-update
  8.0 0.7 all-gather.6.cloned.1.call-update
  8.9 0.7 all-gather.10.cloned.1.call-update
  9.7 0.6 all-gather.12.cloned.1.call-update
  10.4 0.2 copy.38
  10.6 20.9 %all-gather = s32[3072,2]{0,1:T(2,128)S(1)} all-gather(s32[384,2]{0,1:T(2,128)S(1)} %copy-done.11), channel_id=2, replica_groups=mesh['dp'=2,'wg'=8] {'wg'}, dimensions={0}, use_global_device_ids=true | all-gather | bytes 27648 | tf_op jit(solution)/shard_map/all_gather | solution.py:529
  31.5 0.6 copy.44
  32.1 27.7 %all_gather.21 = bf16[4096,12]{1,0:T(8,128)(2,1)S(1)} all-gather(bf16[512,12]{1,0:T(8,128)(2,1)S(1)} %copy.38), channel_id=1, replica_groups=mesh['dp'=2,'wg'=8] {'wg'}, dimensions={0}, use_global_device_ids=true | all-gather | bytes 110592 | tf_op jit(solution)/shard_map/all_gather | solution.py:526
  59.8 1.2 pad.4.wr
  61.0 0.7 fusion.22
  61.7 0.3 fusion.28
  62.0 2.8 convert_reduce_fusion
  64.8 2.6 fusion.24
  67.5 305.1 %reshard.1 = (bf16[8,4096,256]{2,1,0:T(8,128)(2,1)}, bf16[8,1024,512]{2,1,0:T(8,128)(2,1)}, bf16[2,2,2,512,256]{4,3,2,1,0:T(8,128)(2,1)}, bf16[2,2,2,128,512]{4,3,2,1,0:T(8,128)(2,1)}) custom-call(bf16[8,512,1024]{2,1,0:T(8,128)(2,1)} %gate.1, bf16[8,512,1024]{2,1,0:T(8,128)(2,1)} %up.1, bf16[8,128,4096]{2,1,0:T(8,128)(2,1)} %down.1), custom_call_target="tpu_custom_call" | custom-call | flops 99999997952 | bytes 50000000 | tf_op jit(solution)/shard_map/reshard/pallas_call | solution.py:237
  372.7 6.0 convert_bitcast_fusion.1
  378.7 0.3 copy.54
  379.1 7.7 fusion.26
  386.8 0.2 copy.53
  387.0 0.6 subtract_convert_fusion.1
  387.6 1.3 pad_maximum_fusion.1
  388.9 18.0 %convert_bitcast_fusion = f32[48,8,32,128]{3,1,2,0:T(8,128)S(1)} fusion(bf16[384,4096]{1,0:T(8,128)(2,1)} %fusion.24, bf16[4096,4096]{1,0:T(8,128)(2,1)} %all-gather.10.cloned.1.call-done), kind=kOutput, calls=%fused_computation.38 | convolution fusion | flops 12888047616 | bytes 42991616 | tf_op jit(solution)/shard_map/dot_general | solution.py:22
  406.9 1.3 copy.55
  408.2 2.7 subtract_convert_fusion
  410.9 1.2 copy.39
  412.1 1.2 copy.40
  413.3 3.4 pad_maximum_fusion
  416.7 31.4 %while.12 = (s32[]{:T(128)}, bf16[3,128,8,4,128]{4,3,2,1,0:T(4,128)(2,1)}, bf16[3,128,8,128]{3,2,1,0:T(8,128)(2,1)S(1)}, s32[3]{0:T(128)S(1)}, bf16[3,128,8,128]...) while((s32[]{:T(128)}, bf16[3,128,8,4,128]{4,3,2,1,0:T(4,128)(2,1)}, ...), condition=%wide.region_4.5_spmd, body=%wide.region_1.4_spmd.sunk | while | flops 272662784 | bytes 12649825 | solution.py:67
  416.7 1.0 constant_dynamic-slice_fusion.3
  417.7 0.6 dynamic_slice.44
  418.3 0.6 iota_compare_fusion.3
  419.0 3.6 fusion.49
  422.6 0.2 copy.68
  422.8 2.0 fusion.50
  424.9 1.0 copy.69
  425.8 1.3 constant_dynamic-update-slice_fusion.2
  427.2 1.0 constant_dynamic-slice_fusion.3
  428.2 0.6 dynamic_slice.44
  428.8 0.6 iota_compare_fusion.3
  429.4 0.1 fusion.48
  429.5 3.6 fusion.49
  433.1 0.2 copy.68
  433.3 2.0 fusion.50
  435.3 1.0 copy.69
  436.3 1.3 constant_dynamic-update-slice_fusion.2
  437.6 1.0 constant_dynamic-slice_fusion.3
  438.6 0.6 dynamic_slice.44
  439.3 0.6 iota_compare_fusion.3
  439.9 0.1 fusion.48
  440.0 3.6 fusion.49
  443.5 0.2 copy.68
  443.8 2.0 fusion.50
  445.8 1.0 copy.69
  446.8 1.3 constant_dynamic-update-slice_fusion.2
  448.1 0.9 copy-done.4
  449.0 6.2 reshape.170
  455.2 80.2 %all-gather.12.cloned.1.call-done = bf16[4096,4096]{1,0:T(8,128)(2,1)} async-done(((bf16[512,4096]{1,0:T(8,128)(2,1)}), bf16[4096,4096]{1,0:T(8,128)(2,1)}) %all-gather.12.cloned.1.call-update) | async-done | bytes 33554448 | tf_op jit(solution)/shard_map/all_gather | solution.py:540
  535.4 21.9 %multiply_reduce_fusion.1 = (f32[384]{0:T(512)S(1)}, f32[384,4096]{1,0:T(8,128)}) fusion(bf16[384,4096]{1,0:T(8,128)(2,1)} %reshape.170, bf16[4096,4096]{1,0:T(8,128)(2,1)} %all-gather.12.cloned.1.call-done), kind=kOutput, calls=%fused_computation.40 | convolution fusion | flops 12888047616 | bytes 42993152 | tf_op jit(solution)/shard_map/dot_general | solution.py:22
  557.4 4.6 fusion.17
  562.1 2.8 fusion.19
  564.8 1.9 broadcast_in_dim.62.route
  566.7 288.7 %moe.1 = (f32[3,128,4096]{2,1,0:T(8,128)}, bf16[3,8,128,4096]{3,2,1,0:T(8,128)(2,1)}, f32[3,2,128,512]{3,2,1,0:T(8,128)}) custom-call(bf16[3,128,4096]{2,1,0:T(8,128)(2,1)} %bitcast.106, bf16[3,8,2,128,128]{4,3,2,1,0:T(8,128)(2,1)} %broadcast_in_dim.62.route, bf16[4096,128]{1,0:T(8,128)(2,1)} %pad.4.wr, bf16[8,4096,256]{2,1,0:T(8,128)(2,1)} %get-tuple-element.84.wgu, ...), custom_call_target="tpu_custom_call" | custom-call | flops 76999999488 | bytes 100000000 | tf_op jit(solution)/shard_map/moe/pallas_call | solution.py:485
  855.4 3.4 multiply_reduce_fusion
  858.8 0.2 copy-done.3
  859.1 5.9 fusion.20
  (53 shorter events, 0.6 us)
Async XLA Ops:
  7.2 365.5 %all-gather.8.cloned.1.call-start = ((), (), s32[]{:S(2)}) async-start(), calls=%async_computation.1 | async-start | bytes 9437184 | tf_op jit(solution)/shard_map/all_gather | solution.py:537
  8.0 371.1 %all-gather.6.cloned.1.call-start = ((), (), s32[]{:S(2)}) async-start(), calls=%async_computation | async-start | bytes 9437184 | tf_op jit(solution)/shard_map/all_gather | solution.py:538
  8.8 380.1 %all-gather.10.cloned.1.call-start = ((), (), s32[]{:S(2)}) async-start(), calls=%async_computation.2 | async-start | bytes 37748736 | tf_op jit(solution)/shard_map/all_gather | solution.py:536
  9.6 0.7 copy-start.12
  9.6 0.7 copy-start.13
  9.6 0.8 copy-start.14
  9.6 0.8 copy-start.15
  9.6 0.8 copy-start.10
  9.6 1.0 copy-start.11
  9.6 51.4 %copy-start = (bf16[3,128,4096]{2,1,0:T(8,128)(2,1)S(1)}, bf16[3,128,4096]{2,1,0:T(8,128)(2,1)}, u32[]{:S(2)}) copy-start(bf16[3,128,4096]{2,1,0:T(8,128)(2,1)} %param.17) | copy-start | bytes 9437188
  9.7 525.8 %all-gather.12.cloned.1.call-start = ((), (), s32[]{:S(2)}) async-start(), calls=%async_computation.3 | async-start | bytes 37748736 | tf_op jit(solution)/shard_map/all_gather | solution.py:540
  67.5 305.2 %copy-start.5 = (bf16[384,4096]{1,0:T(8,128)(2,1)S(1)}, bf16[384,4096]{1,0:T(8,128)(2,1)}, u32[]{:S(2)}) copy-start(bf16[384,4096]{1,0:T(8,128)(2,1)} %fusion.24) | copy-start | bytes 9437188
  413.3 3.4 copy-start.16
  448.1 0.9 copy-start.4
  455.2 102.2 %copy-start.1 = (bf16[3,128,4096]{2,1,0:T(8,128)(2,1)S(1)}, bf16[3,128,4096]{2,1,0:T(8,128)(2,1)}, u32[]{:S(2)}) copy-start(bf16[3,128,4096]{2,1,0:T(8,128)(2,1)} %param.17) | copy-start | bytes 9437188
  455.2 102.2 %copy-start.8 = (f32[4096]{0:T(1024)S(1)}, f32[4096]{0:T(1024)}, u32[]{:S(2)}) copy-start(f32[4096]{0:T(1024)} %get-tuple-element.107) | copy-start | bytes 49156
  557.4 4.6 copy-start.7
  562.0 2.8 copy-start.2
  562.0 2.8 copy-start.9
  855.4 3.7 copy-start.3
  855.4 3.7 copy-start.6
Sparse Core Ops, SparseCore 0:
  9.6 55.4 all-gather.7
  66.7 79.7 all-gather.5
  148.1 232.9 all-gather.9
  382.5 152.8 all-gather.11

commit v2 on v1

--- a/solution.py
+++ b/solution.py
@@ -32,40 +32,8 @@
     half_dim = HEAD_DIM // 2
     inv_freq = ROPE_BASE ** (-jnp.arange(half_dim, dtype=jnp.float32) * (2.0 / HEAD_DIM))
     angles = jnp.arange(seq_len, dtype=jnp.float32)[:, None] * inv_freq[None, :]
-    return jnp.cos(angles)[:, None, :], jnp.sin(angles)[:, None, :]
-
-
-def apply_rope(values, cos_t, sin_t):
-    half_dim = HEAD_DIM // 2
-    values_f32 = values.astype(jnp.float32)
-    first_half = values_f32[..., :half_dim]
-    second_half = values_f32[..., half_dim:]
-    return jnp.concatenate([first_half * cos_t - second_half * sin_t, second_half * cos_t + first_half * sin_t], axis=-1).astype(jnp.bfloat16)
-
-
-def attend_prompt(operands):
-    q_rows, k_rows, v_rows, length = operands
-    positions = jnp.arange(q_rows.shape[0])
-    scores = jnp.einsum('qkgd,skd->kgqs', q_rows, k_rows, preferred_element_type=jnp.float32) * ATTN_SCALE
-    scores = SOFT_CAP * jnp.tanh(scores / SOFT_CAP)
-    allowed = (positions[None, :] <= positions[:, None]) & (positions[None, :] < length)
-    scores = jnp.where(allowed, scores, -1e30)
-    attn_probs = jax.nn.softmax(scores, axis=-1).astype(jnp.bfloat16)
-    return jnp.einsum('kgqs,skd->qkgd', attn_probs, v_rows, preferred_element_type=jnp.float32).astype(jnp.bfloat16)
-
-
-def attend_rows(q_proj, k_proj, v_proj, seq_lens):
-    n_prompts = seq_lens.shape[0]
-    seq_len = q_proj.shape[0] // n_prompts
-    n_heads = q_proj.shape[1] // HEAD_DIM
-    n_kv = k_proj.shape[1] // HEAD_DIM
-    cos_t, sin_t = rope_tables(seq_len)
-    q_rope = apply_rope(q_proj.reshape(n_prompts, seq_len, n_heads, HEAD_DIM), cos_t, sin_t)
-    k_rope = apply_rope(k_proj.reshape(n_prompts, seq_len, n_kv, HEAD_DIM), cos_t, sin_t)
-    v_heads = v_proj.reshape(n_prompts, seq_len, n_kv, HEAD_DIM)
-    q_groups = q_rope.reshape(n_prompts, seq_len, n_kv, n_heads // n_kv, HEAD_DIM)
-    context = lax.map(attend_prompt, (q_groups, k_rope, v_heads, seq_lens))
-    return context.reshape(n_prompts * seq_len, n_heads * HEAD_DIM), k_rope, v_heads
+    cos_t, sin_t = jnp.cos(angles), jnp.sin(angles)
+    return jnp.concatenate([cos_t, cos_t], axis=1), jnp.concatenate([-sin_t, sin_t], axis=1)
 
 
 class Place:
@@ -115,7 +83,7 @@
 
 def enter(place, with_twin):
     barrier = pltpu.get_barrier_semaphore()
-    peers = [(place.dp, place.at(off, rel)) for off in DIRS for rel in (0, 1)] + [(place.dp, place.at(0, 1))]
+    peers = [(place.dp, place.at(off, rel)) for off in (1, -1, 2) for rel in (0, 1)] + [(place.dp, place.at(0, 1))]
     if with_twin:
         peers.append((place.twin, place.me))
     for dp, wg in peers:
@@ -123,133 +91,392 @@
     pl.semaphore_wait(barrier, len(peers))
 
 
-def reshard_kernel(n, gate, up, down, wgu, wd, relay_gu, relay_d, send_sems, recv_sems, loc_sems):
+class Reshard:
+    def __init__(self, wires, gate, up, down, wgu, wd, relay_gu, relay_d, loc_sems):
+        self.wires, self.place = wires, wires.place
+        n = self.place.n
+        self.gate, self.up, self.down, self.wgu, self.wd = gate, up, down, wgu, wd
+        self.relay_gu, self.relay_d, self.loc_sems = relay_gu, relay_d, loc_sems
+        self.experts, self.rows, self.cols = gate.shape[0], gate.shape[1], gate.shape[2] // n
+        self.drows, self.dcols = down.shape[1], down.shape[2] // n
+        self.half, self.quarter = self.experts // 2, self.experts // 4
+        self.mine = self.place.parity * self.half
+        self.theirs = self.half - self.mine
+
+    def piece(self, arr, e0, cnt, j):
+        if arr == 'd':
+            return self.down.at[pl.ds(e0, cnt), :, pl.ds(pl.multiple_of(j * self.dcols, LANES), self.dcols)]
+        ref = self.gate if arr == 'g' else self.up
+        return ref.at[pl.ds(e0, cnt), :, pl.ds(pl.multiple_of(j * self.cols, LANES), self.cols)]
+
+    def land(self, arr, e0, cnt, src):
+        if arr == 'd':
+            return self.wd.at[pl.ds(e0, cnt), pl.ds(pl.multiple_of(src * self.drows, self.drows), self.drows), :]
+        row = pl.ds(pl.multiple_of(src * self.rows, self.rows), self.rows)
+        if arr == 'gu':
+            return self.wgu.at[pl.ds(e0, cnt), row, :]
+        return self.wgu.at[pl.ds(e0, cnt), row, pl.ds(0 if arr == 'g' else self.cols, self.cols)]
+
+    def relay(self, arr, side, rel):
+        if arr == 'd':
+            return self.relay_d.at[side, rel]
+        if arr == 'gu':
+            return self.relay_gu.at[side, rel]
+        return self.relay_gu.at[side, rel, :, :, pl.ds(0 if arr == 'g' else self.cols, self.cols)]
+
+    def span(self, arr):
+        return (self.mine, self.half) if arr == 'd' else (0, self.experts)
+
+    def near(self):
+        me, sib = self.place.me, self.place.at(0, 1)
+        self.local = []
+        for i, arr in enumerate('gud'):
+            e0, cnt = self.span(arr)
+            self.wires.send(('sib', arr), self.piece(arr, e0, cnt, sib), self.land(arr, e0, cnt, me), wg=sib)
+            desc = pltpu.make_async_copy(self.piece(arr, e0, cnt, me), self.land(arr, e0, cnt, me), self.loc_sems.at[i])
+            desc.start()
+            self.local.append(desc)
+
+    def direct(self, rel, arrs):
+        for arr in arrs:
+            for d in DIRS:
+                to = self.place.at(d, rel)
+                self.wires.send(('direct', d, rel, arr), self.piece(arr, self.mine, self.half, to),
+                                self.land(arr, self.mine, self.half, self.place.me), wg=to)
+
+    def first_leg(self, rel, arrs):
+        for arr in arrs:
+            for side, d in enumerate(DIRS):
+                e0 = self.mine + side * self.quarter
+                self.wires.send(('leg1', d, rel, arr), self.piece(arr, e0, self.quarter, self.place.at(2 * d, rel)),
+                                self.relay(arr, side, rel), wg=self.place.at(d, 0))
+
+    def to_twin(self, name, arr, e0, cnt, src):
+        if arr != 'd':
+            region = self.land(arr, e0, cnt, src)
+            self.wires.send(name, region, region, dp=self.place.twin)
+
+    def direct_in(self, rel):
+        for arr in ('gu', 'd'):
+            for d in DIRS:
+                src = self.place.at(-d, rel)
+                for part in arr:
+                    self.wires.recv(('direct', d, rel, part), self.land(part, self.mine, self.half, src))
+                self.to_twin(('twin', d, rel, arr), arr, self.mine, self.half, src)
+
+    def second_leg(self, rel):
+        for arr in ('gu', 'd'):
+            for side, d in enumerate(DIRS):
+                for part in arr:
+                    self.wires.recv(('leg1', d, rel, part), self.relay(part, side, rel))
+                self.wires.send(('leg2', d, rel, arr), self.relay(arr, side, rel),
+                                self.land(arr, self.mine + side * self.quarter, self.quarter, self.place.at(-d, 0)),
+                                wg=self.place.at(d, rel))
+
+    def far_in(self):
+        for arr in ('gu', 'd'):
+            for rel in (0, 1):
+                for side, d in enumerate(DIRS):
+                    src = self.place.at(2 * d, rel)
+                    e0 = self.mine + side * self.quarter
+                    self.wires.recv(('leg2', d, rel, arr), self.land(arr, e0, self.quarter, src))
+                    self.to_twin(('twin2', d, rel, arr), arr, e0, self.quarter, src)
+
+    def finish(self):
+        for arr in 'gud':
+            e0, cnt = self.span(arr)
+            self.wires.recv(('sib', arr), self.land(arr, e0, cnt, self.place.at(0, 1)))
+        for rel in (0, 1):
+            for side, d in enumerate(DIRS):
+                self.wires.recv(('twin', d, rel, 'gu'), self.land('gu', self.theirs, self.half, self.place.at(-d, rel)))
+                self.wires.recv(('twin2', d, rel, 'gu'),
+                                self.land('gu', self.theirs + side * self.quarter, self.quarter, self.place.at(2 * d, rel)))
+        for desc in self.local:
+            desc.wait()
+
+
+class PairGather:
+    def __init__(self, wires, name, src, dst):
+        self.wires, self.place, self.name, self.src, self.dst = wires, wires.place, name, src, dst
+        rows = src.shape[0]
+        self.rows = rows
+        self.given = rows * 5 // 16
+        self.reach = rows - self.given
+        parity = self.place.parity
+        self.start_row = parity * self.given
+        self.give_row = parity * self.reach
+        self.take_row = self.reach - self.give_row
+
+    def part(self, owner, row, cnt):
+        return self.dst.at[owner, pl.ds(pl.multiple_of(row, 16), cnt), :]
+
+    def line(self, owner):
+        return self.part(owner, self.start_row, self.reach)
+
+    def half(self, owner, side):
+        return self.part(owner, self.start_row + side * (self.reach // 2), self.reach // 2)
+
+    def start(self):
+        place, me = self.place, self.place.me
+        own = self.src.at[pl.ds(pl.multiple_of(self.start_row, 16), self.reach), :]
+        for d in DIRS:
+            self.wires.send((self.name, 'own', d), own, self.line(me), wg=place.at(d, 0))
+        self.wires.send((self.name, 'own', 0), self.src, self.dst.at[me], wg=place.at(0, 1))
+
+    def give(self, tag, owner):
+        part = self.part(owner, self.give_row, self.given)
+        self.wires.send((self.name, 'give', tag), part, part, dp=self.place.twin)
+
+    def near_in(self):
+        place = self.place
+        for side, d in enumerate(DIRS):
+            owner = place.at(-d, 0)
+            self.wires.recv((self.name, 'own', d), self.line(owner))
+            far = self.half(owner, side)
+            self.wires.send((self.name, 'far', d), far, far, wg=place.at(d, 0))
+            self.give(d, owner)
+            self.wires.send((self.name, 'across', d), self.line(owner), self.line(owner), wg=place.at(0, 1))
+
+    def far_in(self):
+        place = self.place
+        owner = place.at(2, 0)
+        for side, d in enumerate(DIRS):
+            part = self.half(owner, side)
+            self.wires.recv((self.name, 'far', d), part)
+            self.wires.send((self.name, 'across2', d), part, part, wg=place.at(0, 1))
+        self.give(2, owner)
+
+    def twin_in(self, tags):
+        for tag in tags:
+            part = self.part(self.place.at(-tag, 0), self.take_row, self.given)
+            self.wires.recv((self.name, 'give', tag), part)
+            self.wires.send((self.name, 'across3', tag), part, part, wg=self.place.at(0, 1))
+
+    def sib_in(self):
+        place = self.place
+        self.wires.recv((self.name, 'own', 0), self.dst.at[place.at(0, 1)])
+        for side, d in enumerate(DIRS):
+            self.wires.recv((self.name, 'across', d), self.line(place.at(-d, 1)))
+            self.wires.recv((self.name, 'across2', d), self.half(place.at(2, 1), side))
+        for tag in (1, -1, 2):
+            self.wires.recv((self.name, 'across3', tag), self.part(place.at(-tag, 1), self.take_row, self.given))
+
+
+def attention_kernel(n, experts, hidden, small, mask, cos_t, sin_t, wq, wk, wv, wo, gate, up, down,
+                     x1, h2, k_out, v_out, small_all, gq, gk, gv, go, wgu, wd, relay_gu, relay_d,
+                     h, acc, ctx, wbuf, send_sems, recv_sems, loc_sems, load_sems):
     place = Place(n)
     wires = Wires(place, send_sems, recv_sems)
-    experts, rows, cols = gate.shape[0], gate.shape[1], gate.shape[2] // n
-    drows, dcols = down.shape[1], down.shape[2] // n
-    half, quarter = experts // 2, experts // 4
-    mine, theirs = place.parity * half, half - place.parity * half
     me = place.me
-
-    def piece(arr, e0, cnt, j):
-        if arr == 'd':
-            return down.at[pl.ds(e0, cnt), :, pl.ds(pl.multiple_of(j * dcols, LANES), dcols)]
-        return (gate if arr == 'g' else up).at[pl.ds(e0, cnt), :, pl.ds(pl.multiple_of(j * cols, LANES), cols)]
-
-    def land(arr, e0, cnt, src):
-        if arr == 'd':
-            return wd.at[pl.ds(e0, cnt), pl.ds(pl.multiple_of(src * drows, drows), drows), :]
-        row = pl.ds(pl.multiple_of(src * rows, rows), rows)
-        if arr == 'gu':
-            return wgu.at[pl.ds(e0, cnt), row, :]
-        return wgu.at[pl.ds(e0, cnt), row, pl.ds(0 if arr == 'g' else cols, cols)]
-
-    def relay(arr, side, rel):
-        if arr == 'd':
-            return relay_d.at[side, rel]
-        if arr == 'gu':
-            return relay_gu.at[side, rel]
-        return relay_gu.at[side, rel, :, :, pl.ds(0 if arr == 'g' else cols, cols)]
+    prompts, seq = mask.shape[0], mask.shape[1]
+    rows, d_model = hidden.shape
+    depth = wq.shape[0]
+    q_dim, kv_dim = wq.shape[1], wk.shape[1]
+    n_kv = kv_dim // HEAD_DIM
+    group = q_dim // kv_dim
+    tile = 512
+    row_tile = seq
 
     enter(place, True)
-    local = []
-    for i, arr in enumerate('gud'):
-        desc = pltpu.make_async_copy(piece(arr, 0, experts, me), land(arr, 0, experts, me), loc_sems.at[i])
-        desc.start()
-        local.append(desc)
-
-    def direct(rel, arrs):
-        for arr in arrs:
-            for d in DIRS:
-                to = place.at(d, rel)
-                wires.send(('direct', d, rel, arr), piece(arr, mine, half, to), land(arr, mine, half, me), wg=to)
-
-    def first_leg(rel, arrs):
-        for arr in arrs:
-            for side, d in enumerate(DIRS):
-                e0 = mine + side * quarter
-                wires.send(('leg1', d, rel, arr), piece(arr, e0, quarter, place.at(2 * d, rel)), relay(arr, side, rel),
-                           wg=place.at(d, 0))
-
-    def to_twin(name, arr, e0, cnt, src):
-        region = land(arr, e0, cnt, src)
-        wires.send(name, region, region, dp=place.twin)
-
-    direct(0, 'gud')
-    sib = place.at(0, 1)
-    for arr in 'gud':
-        wires.send(('sib', arr), piece(arr, 0, experts, sib), land(arr, 0, experts, me), wg=sib)
-    first_leg(0, 'gud')
-    first_leg(1, 'gud')
-    direct(1, 'gud')
-
-    def direct_in(rel, arrs):
-        for arr in arrs:
-            for d in DIRS:
-                src = place.at(-d, rel)
-                if arr == 'gu':
-                    wires.recv(('direct', d, rel, 'g'), land('g', mine, half, src))
-                    wires.recv(('direct', d, rel, 'u'), land('u', mine, half, src))
-                else:
-                    wires.recv(('direct', d, rel, arr), land(arr, mine, half, src))
-                to_twin(('twin', d, rel, arr), arr, mine, half, src)
-
-    def second_leg(rel):
-        for arr in ('gu', 'd'):
-            for side, d in enumerate(DIRS):
-                if arr == 'gu':
-                    wires.recv(('leg1', d, rel, 'g'), relay('g', side, rel))
-                    wires.recv(('leg1', d, rel, 'u'), relay('u', side, rel))
-                else:
-                    wires.recv(('leg1', d, rel, arr), relay(arr, side, rel))
-                wires.send(('leg2', d, rel, arr), relay(arr, side, rel), land(arr, mine + side * quarter, quarter, place.at(-d, 0)),
-                           wg=place.at(d, rel))
-
-    direct_in(0, ('gu', 'd'))
-    second_leg(0)
-    second_leg(1)
-    direct_in(1, ('gu', 'd'))
-    for rel in (0, 1):
-        for arr in ('gu', 'd'):
-            for side, d in enumerate(DIRS):
-                src = place.at(2 * d, rel)
-                e0 = mine + side * quarter
-                wires.recv(('leg2', d, rel, arr), land(arr, e0, quarter, src))
-                to_twin(('twin2', d, rel, arr), arr, e0, quarter, src)
-    for arr in 'gud':
-        wires.recv(('sib', arr), land(arr, 0, experts, sib))
-    for rel in (0, 1):
-        for arr in ('gu', 'd'):
-            for side, d in enumerate(DIRS):
-                wires.recv(('twin', d, rel, arr), land(arr, theirs, half, place.at(-d, rel)))
-                wires.recv(('twin2', d, rel, arr), land(arr, theirs + side * quarter, quarter, place.at(2 * d, rel)))
-    for desc in local:
-        desc.wait()
+    others = [(off, rel) for off in (0, 1, -1, 2) for rel in (0, 1)][1:]
+    for off, rel in others:
+        wires.send(('small', off, rel), small, small_all.at[me], wg=place.at(off, rel))
+    gather_q = PairGather(wires, 'q', wq, gq)
+    gather_k = PairGather(wires, 'k', wk, gk)
+    gather_v = PairGather(wires, 'v', wv, gv)
+    gather_o = PairGather(wires, 'o', wo, go)
+    moving = Reshard(wires, gate, up, down, wgu, wd, relay_gu, relay_d, loc_sems)
+    gather_q.start()
+    gather_k.start()
+    gather_v.start()
+    small_all[me] = small[...]
+    for off, rel in others:
+        wires.recv(('small', off, rel), small_all.at[place.at(-off, rel)])
+
+    def gain(i):
+        return jnp.concatenate([small_all[j, pl.ds(experts + i, 1), :] for j in range(n)], axis=1).astype(jnp.float32)
+
+    def norm(values):
+        return values * lax.rsqrt(jnp.mean(values * values, axis=-1, keepdims=True) + NORM_EPS)
+
+    def norm_in(i, carry):
+        r = pl.ds(pl.multiple_of(i * 16, 16), 16)
+        h[r, :] = (norm(hidden[r, :].astype(jnp.float32)) * gain(0)).astype(jnp.bfloat16)
+        return carry
+
+    lax.fori_loop(0, rows // 16, norm_in, 0)
+    acc[...] = jnp.zeros_like(acc)
+
+    gather_q.near_in()
+    gather_o.start()
+    gather_k.near_in()
+    gather_v.near_in()
+    moving.direct(0, 'gu')
+    moving.near()
+    gather_q.twin_in((1, -1))
+    gather_q.far_in()
+    gather_k.twin_in((1, -1))
+    gather_v.twin_in((1, -1))
+    gather_k.far_in()
+    gather_v.far_in()
+    gather_q.twin_in((2,))
+    gather_k.twin_in((2,))
+    gather_v.twin_in((2,))
+    gather_q.sib_in()
+    gather_k.sib_in()
+    gather_v.sib_in()
+
+    def owner_of(i):
+        return (me + i) % n
+
+    def product(lhs, weights, first_col):
+        def loads(i, slot):
+            owner = owner_of(i)
+
+            def start(own):
+                col = 0
+                for w, (src, gathered) in enumerate(weights):
+                    width = src.shape[1]
+                    pltpu.make_async_copy(src if own else gathered.at[owner], wbuf.at[slot, :, pl.ds(col, width)],
+                                          load_sems.at[slot, w]).start()
+                    col += width
+
+            @pl.when(i == 0)
+            def _():
+                start(True)
+
+            @pl.when(i > 0)
+            def _():
+                start(False)
+
+        def step(i, carry):
+            slot = i % 2
+            owner = owner_of(i)
+
+            @pl.when(i + 1 < n)
+            def _():
+                loads(i + 1, 1 - slot)
+
+            col = 0
+            for w, (src, gathered) in enumerate(weights):
+                width = src.shape[1]
+                pltpu.make_async_copy(gathered.at[owner], wbuf.at[slot, :, pl.ds(col, width)], load_sems.at[slot, w]).wait()
+                col += width
+
+            def tiles(j, carry):
+                c = pl.ds(pl.multiple_of(j * tile, tile), tile)
+                acc[:, c] += dot_f32(lhs[:, pl.ds(pl.multiple_of(owner * depth, depth), depth)], wbuf[slot, :, c])
+                return carry
+
+            return lax.fori_loop(0, col // tile, tiles, carry)
+
+        loads(0, 0)
+        lax.fori_loop(0, n, step, 0)
+
+    product(h, ((wq, gq), (wk, gk), (wv, gv)), 0)
+
+    def rope(values):
+        values = values.astype(jnp.bfloat16).astype(jnp.float32)
+        cos_v, sin_v = cos_t[...], sin_t[...]
+        times = values.shape[0] // seq
+        if times > 1:
+            cos_v, sin_v = jnp.concatenate([cos_v] * times, axis=0), jnp.concatenate([sin_v] * times, axis=0)
+        return (values * cos_v + pltpu.roll(values, HEAD_DIM // 2, 1) * sin_v).astype(jnp.bfloat16)
+
+    def attend(i, carry):
+        p, g = i // n_kv, i % n_kv
+        r = pl.ds(pl.multiple_of(p * seq, seq), seq)
+        kv_cols = pl.ds(pl.multiple_of(g * HEAD_DIM, HEAD_DIM), HEAD_DIM)
+        q = jnp.concatenate([acc[r, pl.ds(pl.multiple_of((g * group + j) * HEAD_DIM, HEAD_DIM), HEAD_DIM)]
+                             for j in range(group)], axis=0)
+        q = rope(q)
+        k = rope(acc[r, pl.ds(pl.multiple_of(q_dim + g * HEAD_DIM, HEAD_DIM), HEAD_DIM)])
+        v = acc[r, pl.ds(pl.multiple_of(q_dim + kv_dim + g * HEAD_DIM, HEAD_DIM), HEAD_DIM)].astype(jnp.bfloat16)
+        k_out[r, kv_cols] = k
+        v_out[r, kv_cols] = v
+        scores = lax.dot_general(q, k, (((1,), (1,)), ((), ())), preferred_element_type=jnp.float32) * ATTN_SCALE
+        scores = SOFT_CAP * jnp.tanh(scores / SOFT_CAP)
+        allowed = jnp.concatenate([mask[p]] * group, axis=0) > 0.5
+        scores = jnp.where(allowed, scores, -1e30)
+        ex = jnp.exp(scores - jnp.max(scores, axis=-1, keepdims=True))
+        probs = (ex / jnp.sum(ex, axis=-1, keepdims=True)).astype(jnp.bfloat16)
+        out = dot_f32(probs, v).astype(jnp.bfloat16)
+        for j in range(group):
+            ctx[r, pl.ds(pl.multiple_of((g * group + j) * HEAD_DIM, HEAD_DIM), HEAD_DIM)] = out[j * seq:(j + 1) * seq]
+        return carry
+
+    lax.fori_loop(0, prompts * n_kv, attend, 0)
+
+    gather_o.near_in()
+    moving.direct(0, 'd')
+    moving.first_leg(0, 'gud')
+    moving.first_leg(1, 'gud')
+    moving.direct(1, 'gud')
+    gather_o.twin_in((1, -1))
+    gather_o.far_in()
+    moving.direct_in(0)
+    gather_o.twin_in((2,))
+    gather_o.sib_in()
+    acc[...] = jnp.zeros_like(acc)
+    product(ctx, ((wo, go),), 0)
+
+    def finish_rows(i, carry):
+        r = pl.ds(pl.multiple_of(i * 16, 16), 16)
+        mid = (hidden[r, :].astype(jnp.float32) + norm(acc[r, pl.ds(0, d_model)]) * gain(1)).astype(jnp.bfloat16)
+        x1[r, :] = mid
+        h2[r, :] = (norm(mid.astype(jnp.float32)) * gain(2)).astype(jnp.bfloat16)
+        return carry
+
+    lax.fori_loop(0, rows // 16, finish_rows, 0)
+    moving.second_leg(0)
+    moving.second_leg(1)
+    moving.direct_in(1)
+    moving.far_in()
+    moving.finish()
     wires.finish()
 
 
-def reshard(n, gate, up, down):
-    experts, rows, ff = gate.shape
-    drows, d_model = down.shape[1:]
+def attention(n, experts, hidden, small, mask, cos_t, sin_t, wq, wk, wv, wo, gate, up, down):
+    rows, d_model = hidden.shape
+    ff = gate.shape[2]
+    drows = down.shape[1]
     cols, dcols = ff // n, d_model // n
-    bf16 = jnp.bfloat16
+    bf16, f32 = jnp.bfloat16, jnp.float32
+    quarter = experts // 4
+
+    def full(w):
+        return jax.ShapeDtypeStruct((n,) + w.shape, bf16)
+
     outs = pl.pallas_call(
-        functools.partial(reshard_kernel, n),
-        name='reshard',
+        functools.partial(attention_kernel, n, experts),
+        name='attention',
         out_shape=(
-            jax.ShapeDtypeStruct((experts, rows * n, 2 * cols), bf16),
+            jax.ShapeDtypeStruct((rows, d_model), bf16),
+            jax.ShapeDtypeStruct((rows, d_model), bf16),
+            jax.ShapeDtypeStruct((rows, wk.shape[1]), bf16),
+            jax.ShapeDtypeStruct((rows, wv.shape[1]), bf16),
+            full(small), full(wq), full(wk), full(wv), full(wo),
+            jax.ShapeDtypeStruct((experts, d_model, 2 * cols), bf16),
             jax.ShapeDtypeStruct((experts, drows * n, dcols), bf16),
-            jax.ShapeDtypeStruct((2, 2, experts // 4, rows, 2 * cols), bf16),
-            jax.ShapeDtypeStruct((2, 2, experts // 4, drows, dcols), bf16),
+            jax.ShapeDtypeStruct((2, 2, quarter, gate.shape[1], 2 * cols), bf16),
+            jax.ShapeDtypeStruct((2, 2, quarter, drows, dcols), bf16),
         ),
-        in_specs=[ANY] * 3,
-        out_specs=(ANY,) * 4,
-        scratch_shapes=[pltpu.SemaphoreType.DMA((64,)), pltpu.SemaphoreType.DMA((64,)), pltpu.SemaphoreType.DMA((4,))],
-        compiler_params=pltpu.CompilerParams(collective_id=0, has_side_effects=True),
-        cost_estimate=pl.CostEstimate(flops=100_000_000_000, bytes_accessed=50_000_000, transcendentals=0),
-    )(gate, up, down)
-    return outs[0], outs[1]
+        in_specs=[VMEM_FULL] * 5 + [ANY] * 7,
+        out_specs=(VMEM_FULL,) * 5 + (ANY,) * 8,
+        scratch_shapes=[
+            pltpu.VMEM((rows, d_model), bf16),
+            pltpu.VMEM((rows, wq.shape[1] + 2 * wk.shape[1]), f32),
+            pltpu.VMEM((rows, wq.shape[1]), bf16),
+            pltpu.VMEM((2, wq.shape[0], wq.shape[1] + 2 * wk.shape[1]), bf16),
+            pltpu.SemaphoreType.DMA((160,)),
+            pltpu.SemaphoreType.DMA((160,)),
+            pltpu.SemaphoreType.DMA((4,)),
+            pltpu.SemaphoreType.DMA((2, 3)),
+        ],
+        compiler_params=pltpu.CompilerParams(collective_id=0, has_side_effects=True, vmem_limit_bytes=62_000_000),
+        cost_estimate=pl.CostEstimate(flops=33_000_000_000, bytes_accessed=300_000_000, transcendentals=0),
+    )(hidden, small, mask, cos_t, sin_t, wq, wk, wv, wo, gate, up, down)
+    return outs[0], outs[1], outs[2], outs[3], outs[4], outs[9], outs[10]
 
 
 class Gather:
@@ -300,7 +527,7 @@
     dcols = vd.shape[2]
     offsets = (0, -1, 1, 2)
 
-    enter(place, False)
+    enter(place, True)
     h_gathers = []
     for t in range(steps):
         gather = Gather(wires, ('h', t), lambda owner, t=t: hg.at[t, owner],
@@ -312,8 +539,13 @@
         desc = pltpu.make_async_copy(wgu.at[e], vgu.at[e], w_sems.at[e])
         desc.start()
         w_loads.append(desc)
-    d_load = pltpu.make_async_copy(wd, vd, w_sems.at[experts])
+    half = experts // 2
+    mine, theirs = place.parity * half, half - place.parity * half
+    own_half, their_half = vd.at[pl.ds(mine, half)], vd.at[pl.ds(theirs, half)]
+    d_load = pltpu.make_async_copy(wd.at[pl.ds(mine, half)], own_half, w_sems.at[experts])
     d_load.start()
+    d_load.wait()
+    wires.send('d', own_half, own_half, dp=place.twin)
 
     def u_owner_chip(owner, q):
         return (owner // 2 + offsets[q] + chips) % chips
@@ -396,7 +628,7 @@
 
     def phase_b(t):
         if t == 0:
-            d_load.wait()
+            wires.recv('d', their_half)
         for q in range(4):
             gather = u_gathers[t, q]
             gather.far_in()
@@ -517,32 +749,29 @@
     row_spec = P(('dp', 'wg'))
     dim0_spec = P('wg', None)
     dim1_spec = P(None, 'wg', None)
-    gather_dim0 = functools.partial(lax.all_gather, axis_name='wg', axis=0, tiled=True)
 
     def device_fn(hidden, seq_lens, route_idx, g_attn_in, w_query, w_key, w_value, w_attn_out, g_attn_out, g_moe_in, w_router, w_gate, w_up, w_down, g_moe_out):
         n_prompts, seq_len, d_model = hidden.shape
         experts = w_router.shape[1]
-        small = jnp.concatenate([w_router] + [g[:, None] for g in (g_attn_in, g_attn_out, g_moe_in, g_moe_out)], axis=1)
-        small = gather_dim0(small)
-        g_attn_in, g_attn_out, g_moe_in, g_moe_out = (small[:, experts + i] for i in range(4))
-        wr = jnp.pad(small[:, :experts], ((0, 0), (0, LANES - experts)))
-        route = lax.all_gather(route_idx, 'wg', axis=0, tiled=False)
-        route = route.reshape(n, n_prompts, seq_len, 2).transpose(1, 0, 3, 2).astype(jnp.bfloat16)
+        rows = n_prompts * seq_len
+        depth = w_query.shape[0]
+        routes = jnp.pad(route_idx.T.astype(jnp.bfloat16), ((0, 0), (0, depth - rows)))
+        small = jnp.concatenate([w_router.T] + [g[None] for g in (g_attn_in, g_attn_out, g_moe_in, g_moe_out)] + [routes], axis=0)
+        small = jnp.pad(small, ((0, -small.shape[0] % 16), (0, 0)))
+        pos = jnp.arange(seq_len)
+        mask = ((pos[None, None, :] <= pos[None, :, None]) & (pos[None, None, :] < seq_lens[:, None, None])).astype(jnp.float32)
+        cos_t, sin_t = rope_tables(seq_len)
+        tok_rows = hidden.reshape(rows, d_model)
+        x1, h2, k_rope, v_rows, small_all, wgu, wd = attention(
+            n, experts, tok_rows, small, mask, cos_t, sin_t, w_query, w_key, w_value, w_attn_out, w_gate, w_up, w_down)
+        wr = jnp.pad(small_all[:, :experts].transpose(0, 2, 1).reshape(d_model, experts), ((0, 0), (0, LANES - experts)))
+        route = small_all[:, experts + 4:experts + 6, :rows].reshape(n, 2, n_prompts, seq_len).transpose(2, 0, 1, 3)
         route = jnp.broadcast_to(route[..., None], route.shape + (LANES,))
-        wgu, wd = reshard(n, w_gate, w_up, w_down)
-
-        tok_rows = hidden.reshape(n_prompts * seq_len, d_model)
-        h_attn = rms_norm(tok_rows, g_attn_in).astype(jnp.bfloat16)
-        q_proj = dot_f32(h_attn, gather_dim0(w_query)).astype(jnp.bfloat16)
-        k_proj = dot_f32(h_attn, gather_dim0(w_key)).astype(jnp.bfloat16)
-        v_proj = dot_f32(h_attn, gather_dim0(w_value)).astype(jnp.bfloat16)
-        context_rows, k_rope, v_heads = attend_rows(q_proj, k_proj, v_proj, seq_lens)
-        attn_out = dot_f32(context_rows, gather_dim0(w_attn_out))
-        mid_rows = (tok_rows.astype(jnp.float32) + rms_norm(attn_out, g_attn_out)).astype(jnp.bfloat16)
-        h_moe = rms_norm(mid_rows, g_moe_in).astype(jnp.bfloat16)
-        moe_out = moe(n, h_moe.reshape(hidden.shape), route, wr, wgu, wd).reshape(tok_rows.shape)
-        y_rows = (mid_rows.astype(jnp.float32) + rms_norm(moe_out, g_moe_out)).astype(jnp.bfloat16)
-        return y_rows.reshape(hidden.shape), k_rope, v_heads
+        gain_out = small_all[:, experts + 3].reshape(-1)
+        moe_out = moe(n, h2.reshape(hidden.shape), route, wr, wgu, wd).reshape(rows, d_model)
+        y_rows = (x1.astype(jnp.float32) + rms_norm(moe_out, gain_out)).astype(jnp.bfloat16)
+        cache = (n_prompts, seq_len, w_key.shape[1] // HEAD_DIM, HEAD_DIM)
+        return y_rows.reshape(hidden.shape), k_rope.reshape(cache), v_rows.reshape(cache)
 
     return jax.shard_map(
         device_fn,

time: 880 us -> 822 us (0.934)
  Pallas kernels: 594 us -> 792 us
  waiting for transfers between devices: 83 us -> 0 us
  matrix products: 70.4 us -> 0 us
  blocking collectives: 48.6 us -> 0 us
  other arithmetic: 33.2 us -> 13.1 us
  between operations: 14.6 us -> 0.7 us
  local copies, waits for them, and re-layouts: 28 us -> 14.8 us
    pallas_call x1, Pallas kernels: 305 us -> 503 us  [attention(): pl.pallas_call(functools.partial(attention_kernel, n, experts), name='att...]
    all_gather x4 -> x0, waiting for transfers between devices: 80.3 us -> none  [the longest x1 80.2 us: device_fn(): attn_out = dot_f32(context_rows, gather_dim0(w_attn_out))]
    dot_general x7 -> x0, matrix products: 59.7 us -> none  [the longest x4 53.6 us: dot_f32(): return jnp.dot(left_op, right_op, preferred_element_type=jnp.float32)]
    all_gather x2 -> x0, blocking collectives: 48.6 us -> none  [the longest x1 27.7 us: device_fn(): small = gather_dim0(small)]
    sub x3 -> x0, matrix products: 10.7 us -> none  [attend_prompt(): attn_probs = jax.nn.softmax(scores, axis=-1).astype(jnp.bfloat16)]
  transfers between devices with their start and end apart: 4 -> 0, of which waited for: 1 -> 0; matrix products, arithmetic and copies ran while one was open for 10% -> 0% of each run, Pallas kernels for 35% -> 0%
where the time goes in v2:
time: 822 us; the launch traced here: 821 us
  Pallas kernels  792 us (96%)
  local copies, waits for them, and re-layouts  14.8 us (2%)
  other arithmetic  13.1 us (2%)
    pallas_call x1, Pallas kernels, attention(): pl.pallas_call(functools.partial(attention_kernel, n, experts), name='att...  503 us
    pallas_call x1, Pallas kernels, moe(): pl.pallas_call(functools.partial(moe_kernel, n, experts), name='moe', out...  289 us

profile of v2, /device:TPU:113, one launch (start us, length us, event | category | flops | bytes accessed | tf_op | source)
XLA Modules:
  0.0 820.7 jit_solution(8922401235512673159)
XLA Ops:
  0.6 0.7 iota_compare_fusion.1
  1.4 0.7 convert_bitcast_fusion
  2.1 0.7 broadcast_in_dim.10
  2.8 0.7 broadcast_in_dim.11
  3.4 0.7 broadcast_in_dim.12
  4.1 0.7 broadcast_in_dim.13
  4.8 0.7 concatenate.9
  5.5 0.6 pad.13.small
  6.2 0.7 and_convert_fusion.mask
  6.9 0.3 fusion.5
  7.1 0.8 pad_maximum_fusion
  7.9 503.1 %attention.1 = (bf16[384,4096]{1,0:T(8,128)(2,1)}, bf16[384,4096]{1,0:T(8,128)(2,1)}, bf16[384,1024]{1,0:T(8,128)(2,1)}, bf16[384,1024]{1,0:T(8,128)(2,1)}, bf16...) custom-call(bf16[384,4096]{1,0:T(8,128)(2,1)} %bitcast.38, ...), custom_call_target="tpu_custom_call" | custom-call | flops 32999999488 | bytes 300000000 | tf_op jit(solution)/shard_map/attention/pallas_call | solution.py:450
  511.0 0.8 slice.9
  511.8 0.9 slice_convert_fusion
  512.7 0.8 slice_bitcast_fusion
  513.5 2.2 copy.23
  515.7 2.2 copy.24
  517.9 0.5 copy.22
  518.4 1.2 pad.14.wr
  519.6 1.8 broadcast_in_dim.14.route
  521.4 289.0 %moe.1 = (f32[3,128,4096]{2,1,0:T(8,128)}, bf16[3,8,128,4096]{3,2,1,0:T(8,128)(2,1)}, f32[3,2,128,512]{3,2,1,0:T(8,128)}) custom-call(bf16[3,128,4096]{2,1,0:T(8,128)(2,1)} %bitcast.39, bf16[3,8,2,128,128]{4,3,2,1,0:T(8,128)(2,1)} %broadcast_in_dim.14.route, bf16[4096,128]{1,0:T(8,128)(2,1)} %pad.14.wr, bf16[8,4096,256]{2,1,0:T(8,128)(2,1)} %get-tuple-element.14.wgu, ...), custom_call_target="tpu_custom_call" | custom-call | flops 76999999488 | bytes 100000000 | tf_op jit(solution)/shard_map/moe/pallas_call | solution.py:717
  810.5 0.0 copy-start
  810.5 3.4 multiply_reduce_fusion
  813.9 1.2 copy-done
  815.1 5.6 fusion.2
  (7 shorter events, 0.1 us)
Async XLA Ops:
  810.5 4.6 copy-start
